TPU v7x, 128 devices: a whole 4x4x4 slice. The times are simulated.
128 devices in a mesh: req: 32 (over x, z, core), seq: 4 (over y).
Axes of the slice: x: 4, y: 4, z: 4, core: 2. Of those that a mesh axis runs over, the one named last changes fastest.
Arguments:
- pool_states: float32 [416, 64, 64, 128], P('req', 'seq'), may hold values from -6 to 6
- inner_window: bfloat16 [416, 3, 4096], P('req', None, 'seq'), may hold values from -6 to 6
- state_window: bfloat16 [416, 3, 256], P('req', None, 'seq'), may hold values from -6 to 6
- move_plan: int32 [416, 2], P('req'), may hold values from 0 to 31, as said below
- active_mask: int32 [416], P('req'), may hold values 0 or 1
- inputs_inner: bfloat16 [32, 2048, 4096], P('req', 'seq'), may hold values from -6 to 6
- inputs_state: bfloat16 [32, 2048, 256], P('req', 'seq'), may hold values from -6 to 6
- gate_rows: bfloat16 [32, 2048, 4096], P('req', 'seq'), may hold values from -6 to 6
- step_raw: bfloat16 [32, 2048, 64], P('req', 'seq'), may hold values from -8 to 60
- lengths: int32 [32], P('req'), may hold values from 4 to 2048
- conv_weight: float32 [4, 4352], replicated, may hold values from -3 to 3
- conv_bias: float32 [4352], replicated, may hold values from -3 to 3
- step_bias: float32 [64], replicated, may hold values from -3.3 to -2.7
- decay_log: float32 [64], replicated, may hold values from -10 to 0
- skip_weight: float32 [64], replicated, may hold values from 0.5 to 1.5
- norm_weight: float32 [4096], replicated, may hold values from 0.25 to 1.75
Outputs:
- new_states: float32 [416, 64, 64, 128], P('req', 'seq')
- new_inner_window: bfloat16 [416, 3, 4096], P('req', None, 'seq')
- new_state_window: bfloat16 [416, 3, 256], P('req', None, 'seq')
- mixer_out: bfloat16 [32, 2048, 4096], P('req', 'seq')
Inputs may be any that keep to these rules, and one draw needn't show every extreme that they name: `move_plan`: every pair of a destination index along req and a slot 0 .. 12 is named exactly once; the rows of one device name one destination at most 1 times, and some destination exactly 1 times.
All inputs are finite; a program needn't handle non-finite values. No bound on the sum of `active_mask` on one device may be relied on, other than what follows from the above.
Results may differ from a plain program's by a relative error of at most 0.0087.
Values may be sent and summed in bfloat16 or wider, within the bound.
A program may use at most 192 MiB of HBM per device.

v0:
```python
import jax
import jax.numpy as jnp
from jax import lax
from jax.sharding import PartitionSpec as P

HEAD_DIM = 64
STATE_DIM = 128
KERNEL = 4
BLOCK_LEN = 256
PREFILLS = 1
INNER_DIM = 4096


EPSILON = 1e-05


def shifted(value, axis, steps):
    count = lax.axis_size(axis)
    leading, last = (max(0, -steps), min(count, count - steps))
    return lax.ppermute(value, axis, [(source, source + steps) for source in range(leading, last)])


def entering(shard, axis, combine, identity):
    peers, index = (lax.axis_size(axis), lax.axis_index(axis))
    everything = jax.tree.map(lambda part: lax.all_gather(part, axis), shard)
    start = jax.tree.map(
        lambda part, zero: jnp.broadcast_to(jnp.asarray(zero, part.dtype), part.shape),
        shard,
        identity,
    )

    def hop(k, before):
        reached = k < index
        new = combine(before, jax.tree.map(lambda part: part[k], everything))
        return jax.tree.map(lambda a, b: jnp.where(reached, a, b), new, before)

    return lax.fori_loop(0, peers, hop, start)


def conv_silu(window, new_rows, weight, bias_values):
    extended = jnp.concatenate([window, new_rows], axis=1).astype(jnp.float32)
    length = new_rows.shape[1]
    running = jnp.zeros(new_rows.shape, jnp.float32) + bias_values
    for offset in range(weight.shape[0]):
        running = running + weight[offset] * extended[:, offset : offset + length]
    return jax.nn.silu(running).astype(jnp.bfloat16)


def block_local(value_rows, write_rows, read_rows, step_rows, decay_rates):
    log_decay = step_rows * decay_rates
    running_log = jnp.cumsum(log_decay, axis=0)
    scores = lax.dot_general(
        read_rows, write_rows, (((1,), (1,)), ((), ())), preferred_element_type=jnp.float32
    )
    log_heads = running_log.T
    log_gaps = log_heads[:, :, None] - log_heads[:, None, :]
    positions = jnp.arange(running_log.shape[0])
    causal = positions[:, None] >= positions[None, :]
    decays = jnp.where(causal, jnp.exp(jnp.where(causal, log_gaps, 0.0)), 0.0)
    weights = (scores[None] * decays * step_rows.T[:, None, :]).astype(jnp.bfloat16)
    intra_part = jnp.einsum("hts,shp->thp", weights, value_rows, preferred_element_type=jnp.float32)
    to_end = jnp.exp(running_log[-1:] - running_log) * step_rows
    scaled = (to_end[:, :, None] * value_rows.astype(jnp.float32)).astype(jnp.bfloat16)
    block_state = jnp.einsum("shp,sn->hpn", scaled, write_rows, preferred_element_type=jnp.float32)
    return (intra_part, block_state, running_log)


def local_parts(value_rows, write_rows, read_rows, step_rows, decay_rates):
    batch_size = value_rows.shape[0]
    block_count = value_rows.shape[1] // BLOCK_LEN

    def to_items(source):
        return source.reshape((batch_size * block_count, BLOCK_LEN) + source.shape[2:])

    def from_items(source):
        return source.reshape((batch_size, block_count) + source.shape[1:])

    def one_item(pieces):
        return block_local(pieces[0], pieces[1], pieces[2], pieces[3], decay_rates)

    results = lax.map(
        one_item,
        (to_items(value_rows), to_items(write_rows), to_items(read_rows), to_items(step_rows)),
    )
    return tuple((from_items(result) for result in results))


def blocked(source):
    return source.reshape(
        (source.shape[0], source.shape[1] // BLOCK_LEN, BLOCK_LEN) + source.shape[2:]
    )


def fold_states(initial, block_states, running_logs):

    def fold_advance(carried, pieces):
        return (jnp.exp(pieces[1][:, -1])[:, :, None, None] * carried + pieces[0], None)

    final_state, unused = lax.scan(
        fold_advance, initial, (jnp.moveaxis(block_states, 1, 0), jnp.moveaxis(running_logs, 1, 0))
    )
    return final_state


def run_states(initial, block_states, running_logs, read_blocks):

    def run_advance(carried, pieces):
        block_state, running_log, read_block = pieces
        inter_part = (
            jnp.einsum(
                "bqn,bhpn->bqhp",
                read_block.astype(jnp.float32),
                carried,
                precision=lax.Precision.HIGHEST,
            )
            * jnp.exp(running_log)[:, :, :, None]
        )
        updated = jnp.exp(running_log[:, -1])[:, :, None, None] * carried + block_state
        return (updated, inter_part)

    final_state, inter_parts = lax.scan(
        run_advance,
        initial,
        (
            jnp.moveaxis(block_states, 1, 0),
            jnp.moveaxis(running_logs, 1, 0),
            jnp.moveaxis(read_blocks, 1, 0),
        ),
    )
    return (final_state, jnp.moveaxis(inter_parts, 0, 1))


def assemble(intra_part, inter_parts, value_rows, skip_own, valid_rows):
    combined = (intra_part + inter_parts).reshape(value_rows.shape) + skip_own[
        :, None
    ] * value_rows.astype(jnp.float32)
    combined = combined * valid_rows[:, :, None, None]
    return combined.astype(jnp.bfloat16).reshape(value_rows.shape[0], value_rows.shape[1], -1)


def gated_norm(payload_array, gate_part, norm_weight):
    gated_rows = payload_array.astype(jnp.float32) * jax.nn.silu(gate_part.astype(jnp.float32))
    norm_scale = lax.rsqrt(jnp.mean(gated_rows * gated_rows, axis=-1, keepdims=True) + EPSILON)
    return (gated_rows * norm_scale * norm_weight).astype(jnp.bfloat16)


def last_rows(raw_rows, positions):

    def pick_rows(source_rows, indices):
        return jnp.take(source_rows, indices, axis=0)

    return jax.vmap(pick_rows)(raw_rows, positions)


def migrate(pool_states, inner_window, state_window, move_plan, active_mask):
    slot_count = pool_states.shape[0]
    peer_count = lax.axis_size("req")
    capacity = (2 * slot_count + peer_count - 1) // peer_count
    keep_flag = active_mask.astype(jnp.float32)
    target_device = move_plan[:, 0]
    target_slot = move_plan[:, 1]
    slot_index = jnp.arange(slot_count, dtype=jnp.int32)
    earlier = (target_device[None, :] == target_device[:, None]) & (
        slot_index[None, :] < slot_index[:, None]
    )
    send_rank = jnp.sum(earlier.astype(jnp.int32), axis=1)
    matches = (target_device[None, None, :] == jnp.arange(peer_count)[:, None, None]) & (
        send_rank[None, None, :] == jnp.arange(capacity)[None, :, None]
    )
    source_slot = jnp.sum(jnp.where(matches, slot_index[None, None, :], 0), axis=2).reshape(-1)
    filled = jnp.any(matches, axis=2).reshape(-1)
    slot_tags = jnp.where(filled, jnp.take(target_slot, source_slot), -1).reshape(
        peer_count, capacity
    )

    def packed(source):
        taken_rows = jnp.take(source, source_slot, axis=0)
        return taken_rows.reshape((peer_count, capacity) + source.shape[1:])

    send_states = packed(pool_states * keep_flag[:, None, None, None])
    send_inner = packed(inner_window.astype(jnp.float32) * keep_flag[:, None, None])
    send_outer = packed(state_window.astype(jnp.float32) * keep_flag[:, None, None])
    got_states, got_inner, got_outer, got_tags = (
        lax.all_to_all(
            send_states.astype(jnp.bfloat16), "req", split_axis=0, concat_axis=0, tiled=True
        ).astype(send_states.dtype),
        lax.all_to_all(
            send_inner.astype(jnp.bfloat16), "req", split_axis=0, concat_axis=0, tiled=True
        ).astype(send_inner.dtype),
        lax.all_to_all(
            send_outer.astype(jnp.bfloat16), "req", split_axis=0, concat_axis=0, tiled=True
        ).astype(send_outer.dtype),
        lax.all_to_all(slot_tags, "req", split_axis=0, concat_axis=0, tiled=True),
    )
    flat_tags = got_tags.reshape(-1)
    arrivals = jnp.arange(flat_tags.shape[0], dtype=jnp.int32)
    chosen = jnp.sum(
        jnp.where(flat_tags[None, :] == slot_index[:, None], arrivals[None, :], 0), axis=1
    )

    def placed(source):
        return jnp.take(source.reshape((-1,) + source.shape[2:]), chosen, axis=0)

    return (
        placed(got_states),
        placed(got_inner).astype(jnp.bfloat16),
        placed(got_outer).astype(jnp.bfloat16),
    )


def combine_carries(earlier_part, later_part):
    return (
        earlier_part[0] * later_part[0],
        later_part[1] + later_part[0][:, :, None, None] * earlier_part[1],
    )


def on_device(
    pool_states,
    inner_window,
    state_window,
    move_plan,
    active_mask,
    inputs_inner,
    inputs_state,
    gate_rows,
    step_raw,
    lengths,
    conv_weight,
    conv_bias,
    step_bias,
    decay_log,
    skip_weight,
    norm_weight,
):
    moved_states, moved_inner, moved_outer = migrate(
        pool_states, inner_window, state_window, move_plan, active_mask
    )
    chain_index = lax.axis_index("seq")
    chain_size = lax.axis_size("seq")
    local_length = inputs_inner.shape[1]
    local_heads = moved_states.shape[1]
    decay_rates = -jnp.exp(decay_log)
    offsets = jnp.arange(KERNEL - 1, dtype=jnp.int32)
    raw_rows = jnp.concatenate([inputs_inner, inputs_state], axis=2)
    earlier_rows = shifted(raw_rows[:, local_length - KERNEL + 1 :], "seq", 1)
    initial, head_inner, head_outer = (
        lax.all_gather(moved_states[:PREFILLS], "seq", axis=1, tiled=True),
        lax.all_gather(moved_inner[:PREFILLS].astype(jnp.float32), "seq", axis=2, tiled=True),
        lax.all_gather(moved_outer[:PREFILLS].astype(jnp.float32), "seq", axis=2, tiled=True),
    )
    first_window = jnp.concatenate([head_inner, head_outer], axis=2).astype(jnp.bfloat16)
    window = jnp.where(chain_index == 0, first_window, earlier_rows)
    mixed_rows = conv_silu(window, raw_rows, conv_weight, conv_bias)
    positions = chain_index * local_length + jnp.arange(local_length, dtype=jnp.int32)
    valid_rows = (positions[None, :] < lengths[:, None]).astype(jnp.float32)
    step_sizes = jax.nn.softplus(step_raw.astype(jnp.float32) + step_bias) * valid_rows[:, :, None]
    value_rows = mixed_rows[:, :, :INNER_DIM].reshape(PREFILLS, local_length, -1, HEAD_DIM)
    write_rows = mixed_rows[:, :, INNER_DIM : INNER_DIM + STATE_DIM]
    read_rows = mixed_rows[:, :, INNER_DIM + STATE_DIM :]
    intra_part, block_states, running_logs = local_parts(
        value_rows, write_rows, read_rows, step_sizes, decay_rates
    )
    local_end = fold_states(jnp.zeros_like(block_states[:, 0]), block_states, running_logs)
    device_decay = jnp.exp(jnp.sum(step_sizes * decay_rates, axis=1))
    every_decay = lax.all_gather(device_decay[None], "seq", axis=0, tiled=True)
    prior_decay, prior_state = entering(
        (device_decay, local_end),
        "seq",
        combine_carries,
        (jnp.ones_like(device_decay), jnp.zeros_like(local_end)),
    )
    incoming = prior_state + prior_decay[:, :, None, None] * initial
    unused_final, inter_parts = run_states(incoming, block_states, running_logs, blocked(read_rows))
    later_mask = jnp.arange(chain_size)[:, None, None] > chain_index
    suffix = jnp.prod(jnp.where(later_mask, every_decay, 1.0), axis=0)
    whole_decay = jnp.prod(every_decay, axis=0)
    window_pos = lengths[:, None] - (KERNEL - 1) + offsets[None, :] - chain_index * local_length
    inside = ((window_pos >= 0) & (window_pos < local_length)).astype(jnp.float32)
    window_term = (
        last_rows(raw_rows, jnp.clip(window_pos, 0, local_length - 1)).astype(jnp.float32)
        * inside[:, :, None]
    )
    state_sum, inner_sum, outer_sum = (
        lax.psum_scatter(
            (local_end * suffix[:, :, None, None]).astype(jnp.bfloat16),
            "seq",
            scatter_dimension=1,
            tiled=True,
        ).astype(jnp.float32),
        lax.psum_scatter(
            window_term[:, :, :INNER_DIM].astype(jnp.bfloat16),
            "seq",
            scatter_dimension=2,
            tiled=True,
        ).astype(jnp.float32),
        lax.psum_scatter(
            window_term[:, :, INNER_DIM:].astype(jnp.bfloat16),
            "seq",
            scatter_dimension=2,
            tiled=True,
        ).astype(jnp.float32),
    )
    own_decay = lax.dynamic_slice_in_dim(whole_decay, chain_index * local_heads, local_heads, 1)
    final_own = state_sum + own_decay[:, :, None, None] * moved_states[:PREFILLS]
    kept_inner = inner_sum.astype(jnp.bfloat16)
    kept_outer = outer_sum.astype(jnp.bfloat16)
    mixer_rows = assemble(intra_part, inter_parts, value_rows, skip_weight, valid_rows)
    mixer_out = gated_norm(mixer_rows, gate_rows, norm_weight)
    new_states = jnp.concatenate([final_own, moved_states[PREFILLS:]], axis=0)
    new_inner = jnp.concatenate([kept_inner, moved_inner[PREFILLS:]], axis=0)
    new_outer = jnp.concatenate([kept_outer, moved_outer[PREFILLS:]], axis=0)
    return (new_states, new_inner, new_outer, mixer_out)


def solution(mesh):
    return jax.shard_map(
        on_device,
        mesh=mesh,
        in_specs=(
            P("req", "seq", None, None),
            P("req", None, "seq"),
            P("req", None, "seq"),
            P("req", None),
            P("req"),
            P("req", "seq", None),
            P("req", "seq", None),
            P("req", "seq", None),
            P("req", "seq", None),
            P("req"),
            P(),
            P(),
            P(),
            P(),
            P(),
            P(),
        ),
        out_specs=(
            P("req", "seq", None, None),
            P("req", None, "seq"),
            P("req", None, "seq"),
            P("req", "seq", None),
        ),
        check_vma=False,
    )
```

profile of v0, /device:TPU:1, one launch (start us, length us, event | category | flops | bytes accessed | tf_op | source)
XLA Modules:
  0.0 446.2 jit_solution(18115954467875149810)
XLA Ops:
  9.9 9.4 %all-to-all-start = ((s32[32,1,1]{2,1,0:T(1,128)}), s32[32,1,1]{2,1,0:T(1,128)S(1)}, u32[]{:S(2)}, u32[]{:S(2)}) async-start(s32[32,1,1]{2,1,0:T(1,128)} %copy.141), calls=%async_computation | async-start | bytes 32768 | tf_op jit(solution)/shard_map/all_to_all | solution.py:193
  19.4 2.5 constant_dynamic-update-slice_fusion.1
  21.9 2.1 copy-done.4
  24.0 3.2 collective-permute-start
  35.9 7.3 %all-reduce = f32[256]{0:T(256)S(1)} all-reduce(f32[256]{0:T(256)S(1)} %exponential_dynamic-update-slice_fusion), channel_id=2, replica_groups=mesh['req'=32,'seq'=4] {'seq'}, use_global_device_ids=true, to_apply=%add | all-reduce | flops 256 | bytes 2048
  43.9 9.7 %all-to-all-start.2 = ((bf16[32,1,3,64]{3,2,1,0:T(4,128)(2,1)}), bf16[32,1,3,64]{3,2,1,0:T(4,128)(2,1)S(1)}, u32[]{:S(2)}, u32[]{:S(2)}) async-start(bf16[32,1,3,64]{3,2,1,0:T(4,128)(2,1)} %copy.148), calls=%async_computation.2 | async-start | bytes 65536 | tf_op jit(solution)/shard_map/all_to_all | solution.py:190
  54.4 6.4 %all-to-all-done.2 = bf16[32,1,3,64]{3,2,1,0:T(4,128)(2,1)S(1)} async-done(((bf16[32,1,3,64]{3,2,1,0:T(4,128)(2,1)}), bf16[32,1,3,64]{3,2,1,0:T(4,128)(2,1)S(1)}, u32[]{:S(2)}, u32[]{:S(2)}) %all-to-all-start.2) | async-done | bytes 12320 | tf_op jit(solution)/shard_map/all_to_all | solution.py:190
  60.8 3.9 all-to-all-start.1
  66.2 9.4 %all_gather.21 = bf16[1,3,256]{1,0,2:T(2,128)(2,1)S(1)} all-gather(bf16[1,3,64]{1,0,2:T(2,128)(2,1)S(1)} %copy.150), channel_id=1, replica_groups=mesh['req'=32,'seq'=4] {'seq'}, dimensions={2}, use_global_device_ids=true | all-gather | bytes 1920 | tf_op jit(solution)/shard_map/all_gather | solution.py:250
  76.5 9.2 %all_gather.20 = bf16[1,3,4096]{2,1,0:T(4,128)(2,1)S(1)} all-gather(bf16[1,3,1024]{2,1,0:T(4,128)(2,1)S(1)} %slice.190), channel_id=1, replica_groups=mesh['req'=32,'seq'=4] {'seq'}, dimensions={2}, use_global_device_ids=true | all-gather | bytes 30720 | tf_op jit(solution)/shard_map/all_gather | solution.py:249
  85.8 3.2 maximum_convert_fusion
  89.0 5.7 %multiply_convert_fusion.5 = bf16[1,512,4352]{2,1,0:T(8,128)(2,1)S(1)} fusion(f32[1,515,4352]{2,1,0:T(8,128)S(1)} %maximum_convert_fusion, f32[4352]{0:T(1024)S(1)} %get-tuple-element.419, f32[4352]{0:T(1024)S(1)} %get-tuple-element.420, f32[4352]{0:T(1024)S(1)} %get-tuple-element.418, f32[4352]{0:T(1024)S(1)} %get-tuple-element.417, f32[4352]{0:T(1024)S(1)} %copy-done.15), kind=kLoop, calls=%fused_computation.82 | loop fusion | flops 28966912 | bytes 40195072 | tf_op jit(solution)/shard_map/convert_element_type | solution.py:46
  94.7 2.9 slice.134
  98.1 12.6 %reshape.760 = bf16[2,256,64,64]{3,2,1,0:T(8,128)(2,1)} reshape(bf16[1,512,4096]{2,1,0:T(8,128)(2,1)} %slice.134) | data formatting | bytes 8388608 | tf_op jit(solution)/shard_map/reshape;reshape | solution.py:73
  110.7 10.5 %copy.153 = bf16[2,256,64,64]{1,3,2,0:T(8,128)(2,1)} copy(bf16[2,256,64,64]{3,2,1,0:T(8,128)(2,1)} %reshape.760) | data formatting | bytes 8388608 | tf_op jit(solution)/shard_map/while | solution.py:81
  121.2 23.2 %while.53 = (s32[]{:T(128)}, f32[2,256,64,64]{1,3,2,0:T(8,128)}, f32[2,64,64,128]{3,2,1,0:T(8,128)}, f32[2,256,64]{1,2,0:T(8,128)S(1)}, bf16[2,256,64,64]{1,3,2,...) while((s32[]{:T(128)}, f32[2,256,64,64]{1,3,2,0:T(8,128)}, ...), condition=%wide.region_7.8_spmd, body=%wide.region_4.7_spmd.sunk | while | flops 852639936 | bytes 29435800 | solution.py:81
  122.5 7.8 %bitcast_dynamic-update-slice_fusion.8 = f32[2,256,64,64]{1,3,2,0:T(8,128)} fusion(f32[2,256,64,64]{1,3,2,0:T(8,128)} %get-tuple-element.663, s32[]{:T(128)} %get-tuple-element.662, f32[64,256]{1,0:T(8,128)S(1)} %bitcast.255, f32[64,256]{1,0:T(8,128)S(1)} %get-tuple-element.631, f32[256,256]{1,0:T(8,128)S(1)} %fusion.82, ...), kind=kOutput, calls=%fused_computation.27.clone.1 | convolution fusion | flops 562036736 | bytes 6816768 | tf_op jit(solution)/shard_map/while/body/eval_jaxpr/hts,shp->thp/dot_general | solution.py:61
  130.6 2.1 bitcast_dynamic-update-slice_fusion.9
  134.1 7.8 %bitcast_dynamic-update-slice_fusion.8 = f32[2,256,64,64]{1,3,2,0:T(8,128)} fusion(f32[2,256,64,64]{1,3,2,0:T(8,128)} %get-tuple-element.663, s32[]{:T(128)} %get-tuple-element.662, f32[64,256]{1,0:T(8,128)S(1)} %bitcast.255, f32[64,256]{1,0:T(8,128)S(1)} %get-tuple-element.631, f32[256,256]{1,0:T(8,128)S(1)} %fusion.82, ...), kind=kOutput, calls=%fused_computation.27.clone.1 | convolution fusion | flops 562036736 | bytes 6816768 | tf_op jit(solution)/shard_map/while/body/eval_jaxpr/hts,shp->thp/dot_general | solution.py:61
  142.2 2.1 bitcast_dynamic-update-slice_fusion.9
  144.5 3.9 while.55
  150.0 3.9 copy.170
  153.9 2.7 copy.198
  157.2 4.0 broadcast_multiply_fusion
  161.2 5.1 %gather_fusion.5 = bf16[32,16,64,128]{3,2,1,0:T(8,128)(2,1)} fusion(bf16[13,16,64,128]{3,2,1,0:T(8,128)(2,1)S(1)} %broadcast_multiply_fusion, s32[1024]{0:T(1024)S(1)} %pad_clamp_fusion.1), kind=kCustom, calls=%fused_computation.5 | custom fusion | bytes 16777344 | tf_op jit(solution)/shard_map/jit(_take)/gather | solution.py:177
  166.2 10.1 %fusion.37 = bf16[32,1,16,64,128]{4,3,2,1,0:T(8,128)(2,1)} fusion(bf16[32,16,64,128]{3,2,1,0:T(8,128)(2,1)} %gather_fusion.5, pred[32]{0:T(512)(128)(4,1)S(1)} %compare_and_fusion.2), kind=kLoop, calls=%fused_computation.71 | loop fusion | flops 4194304 | bytes 16777248 | tf_op jit(solution)/shard_map/convert_element_type | solution.py:185
  176.3 13.4 %all-to-all-start.3 = ((bf16[32,1,16,64,128]{4,3,2,1,0:T(8,128)(2,1)}), bf16[32,1,16,64,128]{4,3,2,1,0:T(8,128)(2,1)}, u32[]{:S(2)}, u32[]{:S(2)}) async-start(bf16[32,1,16,64,128]{4,3,2,1,0:T(8,128)(2,1)} %fusion.37), calls=%async_computation.4 | async-start | bytes 16777216 | tf_op jit(solution)/shard_map/all_to_all | solution.py:184
  191.5 105.4 %all-to-all-done.3 = bf16[32,1,16,64,128]{4,3,2,1,0:T(8,128)(2,1)} async-done(((bf16[32,1,16,64,128]{4,3,2,1,0:T(8,128)(2,1)}), bf16[32,1,16,64,128]{4,3,2,1,0:T(8,128)(2,1)}, u32[]{:S(2)}, u32[]{:S(2)}) %all-to-all-start.3) | async-done | bytes 8388640 | tf_op jit(solution)/shard_map/all_to_all | solution.py:184
  296.9 11.3 %bitcast_convert_fusion = f32[32,16,64,128]{3,2,1,0:T(8,128)} fusion(bf16[32,1,16,64,128]{4,3,2,1,0:T(8,128)(2,1)} %all-to-all-done.3), kind=kLoop, calls=%fused_computation.87 | loop fusion | flops 4194304 | bytes 25165824 | tf_op jit(solution)/shard_map/reshape | solution.py:202
  308.2 9.8 %gather_fusion.6 = f32[13,16,64,128]{3,2,1,0:T(8,128)} fusion(f32[32,16,64,128]{3,2,1,0:T(8,128)} %bitcast_convert_fusion, s32[1024]{0:T(1024)} %copy-done.21), kind=kCustom, calls=%fused_computation.6 | custom fusion | bytes 13631540 | tf_op jit(solution)/shard_map/jit(_take)/gather | solution.py:202
  318.0 7.4 %broadcast_select_fusion.2 = f32[13,16,64,128]{3,2,1,0:T(8,128)} fusion(f32[13,16,64,128]{3,2,1,0:T(8,128)} %gather_fusion.6, pred[13]{0:T(512)(128)(4,1)S(1)} %copy-done.23), kind=kLoop, calls=%fused_computation.94 | loop fusion | flops 1703936 | bytes 13631501 | tf_op jit(solution)/shard_map/jit(_take)/select_n | solution.py:202
  332.8 3.5 pad_maximum_fusion
  336.3 8.5 %while.56 = (s32[]{:T(128)}, f32[1,64]{1,0:T(1,128)S(1)}, f32[1,64,64,128]{3,2,1,0:T(8,128)S(1)}, s32[]{:T(128)}, f32[4,1,64]{2,1,0:T(1,128)S(1)}, /*index=5*/f32[4,1,64,64,128]{4,3,2,1,0:T(8,128)}, s32[]{:T(128)}, s32[]{:T(128)}) while((s32[]{:T(128)}, f32[1,64]{1,0:T(1,128)S(1)}, f32[1,64,64,128]{3,2,1,0:T(8,128)S(1)}, ...), condition=%wide.region_17.18_spmd.clone, body=%wide.region_16.17_spmd.clone.sunk | while | flops 2097348 | bytes 6293111 | solution.py:37
  336.4 2.1 fusion.88
  338.5 2.1 fusion.88
  340.6 2.1 fusion.88
  342.8 2.1 fusion.88
  344.9 25.6 %all-gather.5.cloned.1.call-done = f32[1,64,64,128]{3,2,0,1:T(8,128)} async-done(((f32[1,16,64,128]{3,2,0,1:T(8,128)}), f32[1,64,64,128]{3,2,0,1:T(8,128)}) %all-gather.5.cloned.1.call-update) | async-done | bytes 2097168 | tf_op jit(solution)/shard_map/all_gather | solution.py:248
  370.5 2.5 fusion.46
  373.0 12.0 %while.54 = (s32[]{:T(128)}, f32[1,64,64,128]{3,2,1,0:T(8,128)S(1)}, f32[2,1,256,64,64]{2,4,3,1,0:T(8,128)}, f32[2,1,256,64]{2,3,1,0:T(8,128)S(1)}, f32[2,1,64,6...) while((s32[]{:T(128)}, f32[1,64,64,128]{3,2,1,0:T(8,128)S(1)}, ...), condition=%wide.region_19.20_spmd, body=%wide.region_18.19_spmd.sunk | while | flops 1612709888 | bytes 12912469 | solution.py:121
  373.0 3.8 bitcast_dynamic-update-slice_fusion.11
  376.9 2.0 bitcast_add_fusion.7
  379.0 3.8 bitcast_dynamic-update-slice_fusion.11
  384.9 11.7 %bitcast_add_fusion.3 = f32[2,256,64,64]{1,3,2,0:T(8,128)} fusion(f32[2,256,64,64]{1,3,2,0:T(8,128)} %get-tuple-element.220, f32[2,1,256,64,64]{2,4,3,1,0:T(8,128)} %get-tuple-element.223), kind=kLoop, calls=%fused_computation.88 | loop fusion | flops 2097152 | bytes 25165824 | tf_op jit(solution)/shard_map/add | solution.py:134
  396.6 16.3 %copy.169 = f32[2,256,64,64]{3,2,1,0:T(8,128)} copy(f32[2,256,64,64]{1,3,2,0:T(8,128)} %bitcast_add_fusion.3) | data formatting | bytes 16777216 | tf_op jit(solution)/shard_map/reshape | solution.py:134
  412.9 14.8 %reshape.761 = f32[1,512,4096]{2,1,0:T(8,128)} reshape(f32[2,256,64,64]{3,2,1,0:T(8,128)} %copy.169) | data formatting | bytes 16777216 | tf_op jit(solution)/shard_map/reshape | solution.py:134
  427.7 8.5 %multiply_reduce_fusion = (f32[512]{0:T(512)S(1)}, f32[1,512,4096]{2,1,0:T(8,128)S(1)}) fusion(bf16[1,512,4096]{2,1,0:T(8,128)(2,1)} %param.31, f32[512]{0:T(512)S(1)} %copy-done.17, f32[1,512,4096]{2,1,0:T(8,128)} %reshape.761, bf16[1,512,4352]{2,1,0:T(8,128)(2,1)} %copy-done.3, f32[4096]{0:T(1024)S(1)} %mul.312), kind=kLoop, calls=%fused_computation.90 | loop fusion | flops 29359616 | bytes 25186304 | tf_op jit(solution)/shard_map/reduce_sum | solution.py:143
  436.2 3.5 multiply_convert_fusion.6
  (211 shorter events, 35.0 us)
Async XLA Ops:
  7.2 27.1 %copy-start.29 = (u32[128]{0:T(128)S(1)}, u32[128]{0:T(128)}, u32[]{:S(2)}) copy-start(u32[128]{0:T(128)} %constant.240) | copy-start | bytes 1540
  7.2 14.7 %copy-start.8 = (bf16[1,512,256]{2,1,0:T(8,128)(2,1)S(1)}, bf16[1,512,256]{2,1,0:T(8,128)(2,1)}, u32[]{:S(2)}) copy-start(bf16[1,512,256]{2,1,0:T(8,128)(2,1)} %param.30) | copy-start | bytes 786436
  7.2 23.5 %copy-start.27 = (s32[13]{0:T(128)S(1)}, s32[13]{0:T(128)}, u32[]{:S(2)}) copy-start(s32[13]{0:T(128)} %param.28) | copy-start | bytes 160
  7.2 23.5 %copy-start.9 = (bf16[13,3,1024]{2,0,1:T(8,128)(2,1)S(1)}, bf16[13,3,1024]{2,0,1:T(8,128)(2,1)}, u32[]{:S(2)}) copy-start(bf16[13,3,1024]{2,0,1:T(8,128)(2,1)} %param.25) | copy-start | bytes 239620
  7.2 25.4 %copy-start.20 = (bf16[13,3,64]{2,0,1:T(8,128)(2,1)S(1)}, bf16[13,3,64]{2,0,1:T(8,128)(2,1)}, u32[]{:S(2)}) copy-start(bf16[13,3,64]{2,0,1:T(8,128)(2,1)} %param.26) | copy-start | bytes 14980
  7.2 26.8 %copy-start.10 = (f32[4,4352]{1,0:T(4,128)S(1)}, f32[4,4352]{1,0:T(4,128)}, u32[]{:S(2)}) copy-start(f32[4,4352]{1,0:T(4,128)} %param.34) | copy-start | bytes 208900
  7.2 27.0 %copy-start.28 = (f32[64]{0:T(128)S(1)}, f32[64]{0:T(128)}, u32[]{:S(2)}) copy-start(f32[64]{0:T(128)} %param.37) | copy-start | bytes 772
  7.2 28.2 %copy-start.11 = (bf16[1,512,64]{1,2,0:T(8,128)(2,1)S(1)}, bf16[1,512,64]{1,2,0:T(8,128)(2,1)}, u32[]{:S(2)}) copy-start(bf16[1,512,64]{1,2,0:T(8,128)(2,1)} %param.32) | copy-start | bytes 196612
  7.3 28.2 %copy-start.24 = (f32[64]{0:T(128)S(1)}, f32[64]{0:T(128)}, u32[]{:S(2)}) copy-start(f32[64]{0:T(128)} %param.36) | copy-start | bytes 772
  9.9 34.0 %all-to-all-start = ((s32[32,1,1]{2,1,0:T(1,128)}), s32[32,1,1]{2,1,0:T(1,128)S(1)}, u32[]{:S(2)}, u32[]{:S(2)}) async-start(s32[32,1,1]{2,1,0:T(1,128)} %copy.141), calls=%async_computation | async-start | bytes 32768 | tf_op jit(solution)/shard_map/all_to_all | solution.py:193
  19.3 170.7 %reduce-scatter.12.cloned.1.call-start = ((), (), s32[]{:S(2)}) async-start(), calls=%async_computation.11 | async-start | bytes 81920
  21.9 2.1 copy-start.4
  24.0 61.7 %collective-permute-start = (bf16[1,3,4352]{2,1,0:T(4,128)(2,1)S(1)}, bf16[1,3,4352]{2,1,0:T(4,128)(2,1)S(1)}, u32[]{:S(2)}, u32[]{:S(2)}) collective-permute-start(bf16[1,3,4352]{2,1,0:T(4,128)(2,1)S(1)} %slice.129), channel_id=1, source_target_pairs={{0,1},{1,2},{2,3},{4,5},{5,6},{6,7},{8,9},{9,10},{10,11},{12,13},{... | collective-permute-start | bytes 78344 | tf_op jit(solution)/shard_map/ppermute | solution.py:20
  34.2 1.7 copy-start.16
  43.2 32.5 %copy-start.13 = (f32[4,1,64]{2,1,0:T(1,128)}, f32[4,1,64]{2,1,0:T(1,128)S(1)}, u32[]{:S(2)}) copy-start(f32[4,1,64]{2,1,0:T(1,128)S(1)} %reshape.751) | copy-start | bytes 3076
  43.9 17.0 %all-to-all-start.2 = ((bf16[32,1,3,64]{3,2,1,0:T(4,128)(2,1)}), bf16[32,1,3,64]{3,2,1,0:T(4,128)(2,1)S(1)}, u32[]{:S(2)}, u32[]{:S(2)}) async-start(bf16[32,1,3,64]{3,2,1,0:T(4,128)(2,1)} %copy.148), calls=%async_computation.2 | async-start | bytes 65536 | tf_op jit(solution)/shard_map/all_to_all | solution.py:190
  54.4 34.5 %copy-start.22 = (pred[13]{0:T(512)(128)(4,1)}, pred[13]{0:T(512)(128)(4,1)S(1)}, u32[]{:S(2)}) copy-start(pred[13]{0:T(512)(128)(4,1)S(1)} %compare_and_fusion.3) | copy-start | bytes 43
  54.4 34.5 %copy-start.21 = (s32[1024]{0:T(1024)}, s32[1024]{0:T(1024)S(1)}, u32[]{:S(2)}) copy-start(s32[1024]{0:T(1024)S(1)} %pad_clamp_fusion) | copy-start | bytes 12292
  60.8 14.9 %all-to-all-start.1 = ((bf16[32,1,3,1024]{3,2,1,0:T(4,128)(2,1)}), bf16[32,1,3,1024]{3,2,1,0:T(4,128)(2,1)S(1)}, u32[]{:S(2)}, u32[]{:S(2)}) async-start(bf16[32,1,3,1024]{3,2,1,0:T(4,128)(2,1)} %copy.144), calls=%async_computation.1 | async-start | bytes 524288 | tf_op jit(solution)/shard_map/all_to_all | solution.py:187
  64.8 260.6 %reduce-scatter.8.cloned.1.call-start = ((), (), s32[]{:S(2)}) async-start(), calls=%async_computation.7 | async-start | bytes 1310720 | tf_op jit(solution)/shard_map/reduce_scatter | solution.py:285
  65.5 0.6 copy-start.12
  76.5 12.5 %copy-start.7 = (bf16[13,3,1024]{2,1,0:T(4,128)(2,1)}, bf16[13,3,1024]{2,1,0:T(4,128)(2,1)S(1)}, u32[]{:S(2)}) copy-start(bf16[13,3,1024]{2,1,0:T(4,128)(2,1)S(1)} %select_convert_fusion) | copy-start | bytes 239620
  85.7 3.2 copy-start.15
  94.7 3.4 copy-start.3
  122.5 8.1 %copy-start.2 = (bf16[2,256,64,64]{1,3,2,0:T(8,128)(2,1)S(1)}, bf16[2,256,64,64]{1,3,2,0:T(8,128)(2,1)}, u32[]{:S(2)}) copy-start(bf16[2,256,64,64]{1,3,2,0:T(8,128)(2,1)} %get-tuple-element.677) | copy-start | bytes 12582916 | tf_op jit(solution)/shard_map/while
  134.1 8.1 %copy-start.2 = (bf16[2,256,64,64]{1,3,2,0:T(8,128)(2,1)S(1)}, bf16[2,256,64,64]{1,3,2,0:T(8,128)(2,1)}, u32[]{:S(2)}) copy-start(bf16[2,256,64,64]{1,3,2,0:T(8,128)(2,1)} %get-tuple-element.677) | copy-start | bytes 12582916 | tf_op jit(solution)/shard_map/while
  148.4 8.5 %copy-start = (f32[1,64,64,128]{3,2,1,0:T(8,128)}, f32[1,64,64,128]{3,2,1,0:T(8,128)S(1)}, u32[]{:S(2)}) copy-start(f32[1,64,64,128]{3,2,1,0:T(8,128)S(1)} %get-tuple-element.219) | copy-start | bytes 6291460
  148.4 8.5 %copy-start.5 = (f32[2,1,256,64]{3,2,1,0:T(8,128)}, f32[2,1,256,64]{3,2,1,0:T(8,128)S(1)}, u32[]{:S(2)}) copy-start(f32[2,1,256,64]{3,2,1,0:T(8,128)S(1)} %get-tuple-element.757) | copy-start | bytes 393220
  149.9 177.5 %reduce-scatter.10.cloned.1.call-start = ((), (), s32[]{:S(2)}) async-start(), calls=%async_computation.10 | async-start | bytes 1310720
  156.6 179.7 %all-gather.7.cloned.1.call-start = ((), (), s32[]{:S(2)}) async-start(), calls=%async_computation.9 | async-start | bytes 10485760 | tf_op jit(solution)/shard_map/all_gather | solution.py:25
  176.3 13.5 %copy-start.25 = (f32[64]{0:T(128)S(1)}, f32[64]{0:T(128)}, u32[]{:S(2)}) copy-start(f32[64]{0:T(128)} %param.38) | copy-start | bytes 772
  176.3 13.7 %copy-start.26 = (f32[64]{0:T(128)S(1)}, f32[64]{0:T(128)}, u32[]{:S(2)}) copy-start(f32[64]{0:T(128)} %get-tuple-element.421) | copy-start | bytes 772
  176.3 14.6 %slice-start.1 = ((bf16[13,3,64]{2,1,0:T(4,128)(2,1)}), bf16[12,3,64]{2,1,0:T(4,128)(2,1)S(1)}, s32[]{:S(2)}) async-start(bf16[13,3,64]{2,1,0:T(4,128)(2,1)} %copy-done.12), calls=%async_computation.13 | async-start | bytes 24576 | tf_op jit(solution)/shard_map/slice | solution.py:312
  176.3 120.6 %all-to-all-start.3 = ((bf16[32,1,16,64,128]{4,3,2,1,0:T(8,128)(2,1)}), bf16[32,1,16,64,128]{4,3,2,1,0:T(8,128)(2,1)}, u32[]{:S(2)}, u32[]{:S(2)}) async-start(bf16[32,1,16,64,128]{4,3,2,1,0:T(8,128)(2,1)} %fusion.37), calls=%async_computation.4 | async-start | bytes 16777216 | tf_op jit(solution)/shard_map/all_to_all | solution.py:184
  189.7 180.8 %all-gather.5.cloned.1.call-start = ((), (), s32[]{:S(2)}) async-start(), calls=%async_computation.8 | async-start | bytes 2621440 | tf_op jit(solution)/shard_map/all_gather | solution.py:248
  308.2 9.8 %copy-start.23 = (pred[13]{0:T(512)(128)(4,1)S(1)}, pred[13]{0:T(512)(128)(4,1)}, u32[]{:S(2)}) copy-start(pred[13]{0:T(512)(128)(4,1)} %copy-done.22) | copy-start | bytes 43
  318.0 11.9 %copy-start.6 = (f32[2,1,256,64]{3,2,1,0:T(8,128)S(1)}, f32[2,1,256,64]{3,2,1,0:T(8,128)}, u32[]{:S(2)}) copy-start(f32[2,1,256,64]{3,2,1,0:T(8,128)} %copy-done.5) | copy-start | bytes 393220
  329.9 2.9 slice-start
  332.8 3.5 copy-start.14
  332.8 3.5 copy-start.18
  344.9 25.6 %copy-start.1 = (f32[1,64,64,128]{3,2,1,0:T(8,128)}, f32[1,64,64,128]{3,2,1,0:T(8,128)S(1)}, u32[]{:S(2)}) copy-start(f32[1,64,64,128]{3,2,1,0:T(8,128)S(1)} %get-tuple-element.221) | copy-start | bytes 6291460
  412.9 14.8 %copy-start.17 = (f32[512]{0:T(512)S(1)}, f32[512]{0:T(512)}, u32[]{:S(2)}) copy-start(f32[512]{0:T(512)} %copy-done.16) | copy-start | bytes 6148
  427.7 8.5 %copy-start.19 = (f32[4096]{0:T(1024)S(1)}, f32[4096]{0:T(1024)}, u32[]{:S(2)}) copy-start(f32[4096]{0:T(1024)} %param.39) | copy-start | bytes 49156
Sparse Core Ops, SparseCore 0:
  30.7 19.6 reduce-scatter.11
  150.1 27.3 reduce-scatter.7
  179.8 23.4 reduce-scatter.9
  204.8 84.0 all-gather.6
  327.5 42.8 all-gather.4
where the time goes:
time: 448 us; the launch traced here: 446 us
  waiting for transfers between devices  138 us (31%)
  local copies, waits for them, and re-layouts  102 us (23%)
  other arithmetic  96.7 us (22%)
  starting transfers between devices  40.1 us (9%)
  matrix products  27.7 us (6%)
  blocking collectives  25.9 us (6%)
  between operations  15.9 us (4%)
    all_to_all x1, waiting for transfers between devices, migrate(): lax.all_to_all(send_states.astype(jnp.bfloat16), 'req', split_axis=0, con...  105 us
    reshape x2, local copies, waits for them, and re-layouts, assemble(): (intra_part + inter_parts).reshape(value_rows.shape)  31.1 us
    all_gather x1, waiting for transfers between devices, on_device(): lax.all_gather(moved_states[:PREFILLS], 'seq', axis=1, tiled=True)  25.6 us
    unnamed x72, local copies, waits for them, and re-layouts  18.3 us
    dot_general x2, matrix products, block_local(): jnp.einsum('hts,shp->thp', weights, value_rows, preferred_element_type=jn...  15.6 us
    all_to_all x1, starting transfers between devices, migrate(): lax.all_to_all(send_states.astype(jnp.bfloat16), 'req', split_axis=0, con...  13.4 us
    another operation x1, local copies, waits for them, and re-layouts, to_items(): source.reshape((batch_size * block_count, BLOCK_LEN) + source.shape[2:])  12.6 us
    add x1, other arithmetic, assemble(): intra_part + inter_parts  11.7 us
  transfers between devices with their start and end apart: 10, of which 3 were waited for; matrix products, arithmetic and copies ran while one was open for 34% of the time, Pallas kernels for 0%

commit v1 on v0

v1 whole, which is shorter than its diff:
```python
import functools

import jax
import jax.numpy as jnp
from jax import lax
from jax.experimental import pallas as pl
from jax.experimental.pallas import tpu as pltpu
from jax.sharding import PartitionSpec as P

MESH = pl.DeviceIdType.MESH
ANY = pl.BlockSpec(memory_space=pl.ANY)
VM = pl.BlockSpec(memory_space=pltpu.VMEM)
SM = pl.BlockSpec(memory_space=pltpu.SMEM)
F32 = jnp.float32
BF16 = jnp.bfloat16
I32 = jnp.int32

SLOTS = 13
HEADS = 64
INNER = 4096
SPAN = 512
CHUNK = 128
CHUNKS = SPAN // CHUNK
PAIRS = HEADS // 2
HALF = 528
LOG2E = 1.4426950408889634
EPSILON = 1e-05


def nn(a, b):
    return lax.dot_general(a, b, (((1,), (0,)), ((), ())), preferred_element_type=F32)


def nt(a, b):
    return lax.dot_general(a, b, (((1,), (1,)), ((), ())), preferred_element_type=F32)


def split3(v):
    hi = v.astype(BF16)
    rest = v - hi.astype(F32)
    mid = rest.astype(BF16)
    lo = (rest - mid.astype(F32)).astype(BF16)
    return hi, mid, lo


def silu(v):
    return v / (1.0 + jnp.exp(-v))


def softplus(v):
    u = jnp.exp(-jnp.abs(v))
    series = u * (1.0 - u * (0.5 - u * (1.0 / 3.0 - u * (0.25 - u * 0.2))))
    return jnp.maximum(v, 0.0) + jnp.where(u < 0.02, series, jnp.log(1.0 + u))


def pick_matrix(rows, pair):
    row = lax.rem(lax.broadcasted_iota(I32, (rows, 128), 0), 64)
    lane = lax.broadcasted_iota(I32, (rows, 128), 1)
    head = 2 * pair + (lane >= 64).astype(I32)
    return jnp.where(row == head, 1.0, 0.0).astype(BF16)


def conv_tile(x, taps, bias, rows):
    acc = bias + taps[3:4] * x[16 : 16 + rows]
    for k in range(3):
        acc = acc + taps[k : k + 1] * x[13 + k : 13 + k + rows]
    return silu(acc).astype(BF16)


def exchange_kernel(
    meta, lens, skip, tags, pool, win, xin, xst, step, conv_w, conv_b, step_b, decay,
    out_a, out_b, s0_all, f_in, f_st, f_dt, y_out, read_out, cum_out, pre_out, tot_out, fin_out, kept_out,
    stage, sbuf_a, sbuf_b, rel_a, rel_b, rbuf_a, rbuf_b, xbuf, xsbuf, y_buf, read_buf, cum_buf, st_buf,
    lbuf, tbuf, tagbuf, tag_s, cum3, cumt, dt2, sc_buf, wt_buf, base_buf, pay, pre_buf, fin_buf, kept_buf,
    ffin, ffst, ffdt,
    pool_sem, in_sem, out_sem, one_send, one_recv, two_send, two_recv, tag_send, tag_recv,
    halo_send, halo_recv, lend_send, lend_recv, s0_send, s0_recv, f_send, f_recv,
):
    me = lax.axis_index("req")
    my = lax.axis_index("seq")
    mx, mz, mc = me // 8, (me // 2) % 4, me % 2

    def at(dx, dz, dc):
        return ((mx + dx) % 4) * 8 + ((mz + dz) % 4) * 2 + (mc + dc) % 2

    loads = []
    for k in range(SLOTS):
        cp = pltpu.make_async_copy(pool.at[k], stage.at[k], pool_sem.at[k])
        cp.start()
        loads.append(cp)
    ins = [
        pltpu.make_async_copy(xin, xbuf.at[pl.ds(16, SPAN)], in_sem.at[0]),
        pltpu.make_async_copy(xst, xsbuf.at[pl.ds(16, SPAN)], in_sem.at[1]),
    ]
    for cp in ins:
        cp.start()

    barrier = pltpu.get_barrier_semaphore()
    for r in range(1, 32):
        peer = at(r // 8, (r // 2) % 4, r % 2)
        pl.semaphore_signal(barrier, inc=1, device_id=(peer, my), device_id_type=MESH)
    for r in range(1, 4):
        pl.semaphore_signal(barrier, inc=1, device_id=(me, (my + r) % 4), device_id_type=MESH)
    pl.semaphore_wait(barrier, 34)

    pending = []

    def send(src, dst, ssem, rsem, dev):
        cp = pltpu.make_async_remote_copy(
            src_ref=src, dst_ref=dst, send_sem=ssem, recv_sem=rsem, device_id=dev, device_id_type=MESH
        )
        cp.start()
        return cp

    halo = [
        send(xin.at[pl.ds(SPAN - 16, 16)], xbuf.at[pl.ds(0, 16)], halo_send.at[0], halo_recv.at[0], (me, (my + 1) % 4)),
        send(xst.at[pl.ds(SPAN - 16, 16)], xsbuf.at[pl.ds(0, 16)], halo_send.at[1], halo_recv.at[1], (me, (my + 1) % 4)),
    ]
    firsts = []
    for r in range(1, 4):
        dev = (me, (my + r) % 4)
        firsts.append(send(xin.at[pl.ds(0, 16)], ffin.at[my], f_send.at[r], f_recv.at[r], dev))
        firsts.append(send(xst.at[pl.ds(0, 16)], ffst.at[my], f_send.at[4 + r], f_recv.at[4 + r], dev))
        firsts.append(send(step.at[pl.ds(0, 16)], ffdt.at[my], f_send.at[8 + r], f_recv.at[8 + r], dev))

    for cp in loads:
        cp.wait()

    def fill(dest, half, put):
        slot = meta[dest, 0]
        keep = meta[dest, 1].astype(F32)
        put(0, (stage[slot, pl.ds(512 * half, 512), :] * keep).astype(BF16))
        put(512, (win[slot, pl.ds(16 * half, 16), :].astype(F32) * keep).astype(BF16))

    def fill_a(ref, lead, xd):
        def one(q, carry):
            def put(row, value):
                ref[lead, q, pl.ds(row, value.shape[0]), :] = value

            fill(xd * 8 + q, 0, put)
            return carry

        lax.fori_loop(0, 8, one, 0)

    def fill_b(ref, lead, zd):
        def one(q, carry):
            def put(row, value):
                ref[lead, q, pl.ds(row, value.shape[0]), :] = value

            fill((q // 2) * 8 + zd * 2 + q % 2, 1, put)
            return carry

        lax.fori_loop(0, 8, one, 0)

    phase_a, phase_b = {}, {}
    for d in (2, 1, 3):
        xd = (mx + d) % 4
        fill_a(sbuf_a, xd, xd)
        phase_a[d] = send(sbuf_a.at[xd], rel_a.at[mx], one_send.at[d], one_recv.at[d], (at(d, 0, 0), my))
        zd = (mz + d) % 4
        fill_b(sbuf_b, zd, zd)
        phase_b[d] = send(sbuf_b.at[zd], rel_b.at[mz], one_send.at[4 + d], one_recv.at[4 + d], (at(0, d, 0), my))
    fill_a(rel_a, mx, mx)
    fill_b(rel_b, mz, mz)

    second = []

    def forward(d):
        xs = (mx + 4 - d) % 4
        zs = (mz + 4 - d) % 4
        for e in range(1, 8):
            de, dc = e // 2, e % 2
            sem = d * 8 + e
            zt, xt, ct = (mz + de) % 4, (mx + de) % 4, (mc + dc) % 2
            second.append(
                send(rel_a.at[xs, zt * 2 + ct], rbuf_a.at[xs * 8 + mz * 2 + mc],
                     two_send.at[sem], two_recv.at[sem], (at(0, de, dc), my))
            )
            second.append(
                send(rel_b.at[zs, xt * 2 + ct], rbuf_b.at[mx * 8 + zs * 2 + mc],
                     two_send.at[32 + sem], two_recv.at[32 + sem], (at(de, 0, dc), my))
            )
        rbuf_a[xs * 8 + mz * 2 + mc] = rel_a[xs, mz * 2 + mc]
        rbuf_b[mx * 8 + zs * 2 + mc] = rel_b[zs, mx * 2 + mc]

    forward(0)

    tag_copies = []
    for r in range(1, 32):
        peer = at(r // 8, (r // 2) % 4, r % 2)
        tag_copies.append(
            send(tags.at[peer], tagbuf.at[me], tag_send.at[r], tag_recv.at[r], (peer, my))
        )
    tagbuf[me] = tags[me]

    for cp in ins:
        cp.wait()
    for cp in halo:
        cp.wait()

    @pl.when(my == 0)
    def _():
        xbuf[pl.ds(0, 16), :] = jnp.zeros((16, INNER), BF16)
        xsbuf[pl.ds(0, 16), :] = jnp.zeros((16, 256), BF16)

    st_buf[...] = jnp.zeros_like(st_buf)
    base_buf[...] = jnp.zeros_like(base_buf)
    length = lens[0]

    def chunk_body(k, carry):
        r0 = pl.multiple_of(k * CHUNK, CHUNK)
        pos = my * SPAN + r0 + lax.broadcasted_iota(I32, (CHUNK, HEADS), 0)
        live = ((pos < length) & (pos >= 3)).astype(F32)
        dt = softplus(step[pl.ds(r0, CHUNK), :].astype(F32) + step_b[0:1, :]) * live
        rate = dt * (-LOG2E * jnp.exp(decay[0:1, :]))
        rows = lax.broadcasted_iota(I32, (CHUNK, CHUNK), 0)
        cols = lax.broadcasted_iota(I32, (CHUNK, CHUNK), 1)
        tri = jnp.where(rows >= cols, 1.0, 0.0).astype(BF16)
        hi, mid, lo = split3(rate)
        cum = nn(tri, hi) + nn(tri, mid) + nn(tri, lo)
        cum3[...] = jnp.concatenate(split3(cum), axis=1)
        cumt[...] = jnp.transpose(cum)
        dth = dt.astype(BF16)
        dt2[...] = jnp.concatenate([dth, (dt - dth.astype(F32)).astype(BF16)], axis=1)
        cum_buf[pl.ds(r0, CHUNK), :] = cum + base_buf[0:1, 0:HEADS]
        base_buf[0:1, 0:HEADS] = base_buf[0:1, 0:HEADS] + cum[CHUNK - 1 : CHUNK, :]
        xs_tile = xsbuf[pl.ds(r0, CHUNK + 16), :].astype(F32)
        mixed = conv_tile(xs_tile, conv_w[:, INNER : INNER + 256], conv_b[0:1, INNER : INNER + 256], CHUNK)
        write, read = mixed[:, 0:128], mixed[:, 128:256]
        read_buf[pl.ds(r0, CHUNK), :] = read
        sc_buf[...] = jnp.where(rows >= cols, nt(read, write), 0.0)
        wt_buf[...] = jnp.transpose(write.astype(F32)).astype(BF16)

        def pair_body(i, inner):
            l0 = pl.multiple_of(i * 128, 128)
            lanes = pl.ds(l0, 128)
            x = xbuf[pl.ds(r0, CHUNK + 16), lanes].astype(F32)
            value = conv_tile(x, conv_w[:, lanes], conv_b[0:1, lanes], CHUNK)
            row = lax.rem(lax.broadcasted_iota(I32, (192, 256), 0), 64)
            lane2 = lax.broadcasted_iota(I32, (192, 256), 1)
            sel = jnp.where(row == 2 * i + (lane2 >= 128).astype(I32), 1.0, 0.0).astype(BF16)
            both = nn(cum3[...], sel)
            c1, c2 = both[:, 0:128], both[:, 128:256]
            sc = sc_buf[...]
            w1 = sc * jnp.exp2(jnp.minimum(c1 - cumt[pl.ds(2 * i, 1), :], 0.0))
            w2 = sc * jnp.exp2(jnp.minimum(c2 - cumt[pl.ds(2 * i + 1, 1), :], 0.0))
            low = lax.broadcasted_iota(I32, (CHUNK, 128), 1) < 64
            cp = jnp.where(low, c1, c2)
            vf = value.astype(F32)
            vd = vf * nn(dt2[...], pick_matrix(128, i))
            zero = jnp.zeros_like(vd)
            rhs = jnp.concatenate([jnp.where(low, vd, zero), jnp.where(low, zero, vd)], axis=0).astype(BF16)
            lhs = jnp.concatenate([w1.astype(BF16), w2.astype(BF16)], axis=1)
            state = st_buf[:, lanes]
            lane = lax.broadcasted_iota(I32, (1, 128), 1)
            skip_lane = jnp.where(lane < 64, skip[2 * i], skip[2 * i + 1])
            y = nn(lhs, rhs) + nn(read_buf[pl.ds(r0, CHUNK), :], state.astype(BF16)) * jnp.exp2(cp) + skip_lane * vf
            y_buf[pl.ds(r0, CHUNK), lanes] = y.astype(y_buf.dtype)
            last = cp[CHUNK - 1 : CHUNK, :]
            scaled = (jnp.exp2(last - cp) * vd).astype(BF16)
            st_buf[:, lanes] = jnp.exp2(last) * state + nn(wt_buf[...], scaled)
            return inner

        lax.fori_loop(0, PAIRS, pair_body, 0)
        return carry

    lax.fori_loop(0, CHUNKS, chunk_body, 0)

    cols = lax.broadcasted_iota(I32, (16, SPAN), 1)
    rows = lax.broadcasted_iota(I32, (16, SPAN), 0)
    want = length - 3 - my * SPAN
    sel_in = jnp.where((cols == want + rows) & (rows < 3), 1.0, 0.0).astype(BF16)
    sel_st = jnp.where((cols == want + rows - 3) & (rows >= 3) & (rows < 6), 1.0, 0.0).astype(BF16)
    lst = nn(sel_st, xsbuf[pl.ds(16, SPAN), :])

    def lend_body(i, carry):
        lanes = pl.ds(pl.multiple_of(i * 256, 256), 256)
        lbuf[my, pl.ds(0, 128), lanes] = st_buf[:, lanes].astype(BF16)
        first = jnp.where(i == 0, 1.0, 0.0)
        lbuf[my, pl.ds(128, 16), lanes] = (nn(sel_in, xbuf[pl.ds(16, SPAN), lanes]) + first * lst).astype(BF16)
        return carry

    lax.fori_loop(0, INNER // 256, lend_body, 0)
    tbuf[my] = base_buf[...]
    lends = []
    for r in range(1, 4):
        dev = (me, (my + r) % 4)
        lends.append(send(lbuf.at[my], lbuf.at[my], lend_send.at[r], lend_recv.at[r], dev))
        lends.append(send(tbuf.at[my], tbuf.at[my], lend_send.at[4 + r], lend_recv.at[4 + r], dev))

    outs = []

    def put_out(src, dst, i):
        cp = pltpu.make_async_copy(src, dst, out_sem.at[i])
        cp.start()
        outs.append(cp)

    put_out(y_buf, y_out, 0)
    put_out(read_buf, read_out, 1)
    put_out(cum_buf, cum_out, 2)

    for d in (1, 3, 2):
        phase_a[d].wait_recv()
        phase_b[d].wait_recv()
        forward(d)

    for cp in lends:
        cp.wait()

    tot = [tbuf[c][0:1, 0:HEADS] for c in range(4)]
    zero_row = jnp.zeros((1, HEADS), F32)
    prior_rows, suffix_rows = [], []
    for c in range(4):
        before, after = zero_row, zero_row
        for other in range(c + 1, 4):
            after = after + tot[other]
            before = before + tot[other] * jnp.where(other < my, 1.0, 0.0)
        prior_rows.append(jnp.exp2(before) * jnp.where(c < my, 1.0, 0.0))
        suffix_rows.append(jnp.exp2(after))
    prior_log = zero_row
    whole_log = zero_row
    for c in range(4):
        prior_log = prior_log + tot[c] * jnp.where(c < my, 1.0, 0.0)
        whole_log = whole_log + tot[c]
    factors = jnp.concatenate(prior_rows + suffix_rows + [jnp.exp2(whole_log)] + [zero_row] * 7, axis=0)
    factors3 = jnp.concatenate(split3(factors), axis=1)
    tot_out_rows = jnp.concatenate([prior_log, whole_log] + [zero_row] * 6, axis=0)
    base_buf[:, 0:HEADS] = tot_out_rows

    def pre_body(i, carry):
        lanes = pl.ds(pl.multiple_of(i * 128, 128), 128)
        f = nn(factors3, pick_matrix(192, i))
        acc = f[0:1] * lbuf[0, pl.ds(0, 128), lanes].astype(F32)
        for c in range(1, 4):
            acc = acc + f[c : c + 1] * lbuf[c, pl.ds(0, 128), lanes].astype(F32)
        pre_buf[:, lanes] = acc.astype(BF16)
        return carry

    lax.fori_loop(0, PAIRS, pre_body, 0)

    def fin_body(q, carry):
        i = my * 8 + q
        lanes = pl.ds(pl.multiple_of(i * 128, 128), 128)
        f = nn(factors3, pick_matrix(192, i))
        acc = f[4:5] * lbuf[0, pl.ds(0, 128), lanes].astype(F32)
        kept = lbuf[0, pl.ds(128, 16), lanes].astype(F32)
        for c in range(1, 4):
            acc = acc + f[4 + c : 5 + c] * lbuf[c, pl.ds(0, 128), lanes].astype(F32)
            kept = kept + lbuf[c, pl.ds(128, 16), lanes].astype(F32)
        fin_buf[pl.ds(pl.multiple_of(q * 128, 128), 128), :] = jnp.transpose(acc)
        kept_buf[:, pl.ds(pl.multiple_of(q * 128, 128), 128)] = kept.astype(BF16)
        return carry

    lax.fori_loop(0, 8, fin_body, 0)
    kst = lbuf[0, pl.ds(128, 16), pl.ds(0, 256)].astype(F32)
    for c in range(1, 4):
        kst = kst + lbuf[c, pl.ds(128, 16), pl.ds(0, 256)].astype(F32)
    kept_buf[:, pl.ds(1024, 256)] = kst.astype(BF16)

    for i, ref in enumerate(((pre_buf, pre_out), (base_buf, tot_out), (fin_buf, fin_out), (kept_buf, kept_out))):
        put_out(ref[0], ref[1], 3 + i)

    for cp in firsts:
        cp.wait()
    ffin_own = pltpu.make_async_copy(xin.at[pl.ds(0, 16)], ffin.at[my], in_sem.at[2])
    ffst_own = pltpu.make_async_copy(xst.at[pl.ds(0, 16)], ffst.at[my], in_sem.at[3])
    ffin_own.start()
    ffst_own.start()
    ffdt[my] = step[pl.ds(0, 16), :]
    ffin_own.wait()
    ffst_own.wait()
    put_out(ffin.at[0], f_in, 7)
    put_out(ffst.at[0], f_st, 8)
    put_out(ffdt.at[0], f_dt, 9)

    for cp in tag_copies:
        cp.wait()
    tag_load = pltpu.make_async_copy(tagbuf, tag_s, in_sem.at[4])
    tag_load.start()
    tag_load.wait()

    def source_of(j):
        acc = jnp.int32(0)
        for s in range(32):
            acc = acc + jnp.where(tag_s[s, 0, 0] == j + 1, s, 0)
        return acc

    for d in (1, 2, 3):
        phase_a[d].wait_send()
        phase_b[d].wait_send()
    for cp in second:
        cp.wait()

    src0 = source_of(0)
    pay[my, 0] = rbuf_a[src0]
    pay[my, 1] = rbuf_b[src0]
    s0s = []
    for r in range(1, 4):
        s0s.append(send(pay.at[my], pay.at[my], s0_send.at[r], s0_recv.at[r], (me, (my + r) % 4)))
    for j in range(1, SLOTS):
        src = source_of(j)
        sbuf_a[j // 8, j % 8] = rbuf_a[src]
        sbuf_b[j // 8, j % 8] = rbuf_b[src]
        put_out(sbuf_a.at[j // 8, j % 8], out_a.at[j], 10 + 2 * j)
        put_out(sbuf_b.at[j // 8, j % 8], out_b.at[j], 11 + 2 * j)
    put_out(pay.at[my, 0], out_a.at[0], 10)
    put_out(pay.at[my, 1], out_b.at[0], 11)
    for cp in s0s:
        cp.wait()
    put_out(pay, s0_all, 36)
    for cp in outs:
        cp.wait()


def exchange(meta, lens, skip, tags, pool, win, xin, xst, step, conv_w, conv_b, step_b, decay):
    dma = pltpu.SemaphoreType.DMA
    shape = jax.ShapeDtypeStruct
    out_shape = (
        shape((SLOTS, HALF, 128), BF16),
        shape((SLOTS, HALF, 128), BF16),
        shape((4, 2, HALF, 128), BF16),
        shape((16, INNER), BF16),
        shape((16, 256), BF16),
        shape((16, HEADS), BF16),
        shape((SPAN, INNER), BF16),
        shape((SPAN, 128), BF16),
        shape((SPAN, HEADS), F32),
        shape((128, INNER), BF16),
        shape((8, 128), F32),
        shape((1024, 128), F32),
        shape((16, 1280), BF16),
    )
    scratch = [
        pltpu.VMEM((SLOTS, 1024, 128), F32),
        pltpu.VMEM((4, 8, HALF, 128), BF16),
        pltpu.VMEM((4, 8, HALF, 128), BF16),
        pltpu.VMEM((4, 8, HALF, 128), BF16),
        pltpu.VMEM((4, 8, HALF, 128), BF16),
        pltpu.VMEM((32, HALF, 128), BF16),
        pltpu.VMEM((32, HALF, 128), BF16),
        pltpu.VMEM((SPAN + 16, INNER), BF16),
        pltpu.VMEM((SPAN + 16, 256), BF16),
        pltpu.VMEM((SPAN, INNER), BF16),
        pltpu.VMEM((SPAN, 128), BF16),
        pltpu.VMEM((SPAN, HEADS), F32),
        pltpu.VMEM((128, INNER), F32),
        pltpu.VMEM((4, 144, INNER), BF16),
        pltpu.VMEM((4, 8, 128), F32),
        pltpu.VMEM((32, 1, 128), I32),
        pltpu.SMEM((32, 1, 128), I32),
        pltpu.VMEM((CHUNK, 192), BF16),
        pltpu.VMEM((HEADS, CHUNK), F32),
        pltpu.VMEM((CHUNK, 128), BF16),
        pltpu.VMEM((CHUNK, CHUNK), F32),
        pltpu.VMEM((CHUNK, CHUNK), BF16),
        pltpu.VMEM((8, 128), F32),
        pltpu.VMEM((4, 2, HALF, 128), BF16),
        pltpu.VMEM((128, INNER), BF16),
        pltpu.VMEM((1024, 128), F32),
        pltpu.VMEM((16, 1280), BF16),
        pltpu.VMEM((4, 16, INNER), BF16),
        pltpu.VMEM((4, 16, 256), BF16),
        pltpu.VMEM((4, 16, HEADS), BF16),
        dma((SLOTS,)), dma((5,)), dma((37,)),
        dma((8,)), dma((8,)), dma((64,)), dma((64,)), dma((32,)), dma((32,)),
        dma((2,)), dma((2,)), dma((8,)), dma((8,)), dma((4,)), dma((4,)), dma((12,)), dma((12,)),
    ]
    return pl.pallas_call(
        exchange_kernel,
        out_shape=out_shape,
        in_specs=[SM, SM, SM, VM, ANY, VM, ANY, ANY, VM, VM, VM, VM, VM],
        out_specs=[ANY] * len(out_shape),
        scratch_shapes=scratch,
        compiler_params=pltpu.CompilerParams(
            collective_id=1, has_side_effects=True, vmem_limit_bytes=67043328
        ),
        name="exchange",
    )(meta, lens, skip, tags, pool, win, xin, xst, step, conv_w, conv_b, step_b, decay)


def mixer_kernel(
    lens, skip, y_ref, gate, read_ref, cum_ref, pre, s0_all, tot, f_in, f_st, f_dt, wfirst, wfst,
    conv_w, conv_b, step_b, decay, norm_w, out,
    gated, r0_buf, cum3, rw_buf, sc0_buf, cf3_buf, dtf3_buf, prior3,
):
    my = lax.axis_index("seq")
    k = pl.program_id(0)
    length = lens[0]

    posf = lax.broadcasted_iota(I32, (16, HEADS), 0)
    live = ((posf < length) & (posf < 3)).astype(F32)
    dt = softplus(f_dt[...].astype(F32) + step_b[0:1, :]) * live
    rate = dt * (-LOG2E * jnp.exp(decay[0:1, :]))
    c0 = rate[0:1]
    c1 = c0 + rate[1:2]
    c2 = c1 + rate[2:3]
    cumf = jnp.concatenate([c0, c1, c2] + [c2] * 13, axis=0)
    e_st = jnp.concatenate([wfst[...], f_st[...]], axis=0).astype(F32)
    mixed = conv_tile(e_st, conv_w[:, INNER : INNER + 256], conv_b[0:1, INNER : INNER + 256], 16)
    write0, read0 = mixed[:, 0:128], mixed[:, 128:256]
    sc0_buf[...] = nt(read0, write0)
    rw_buf[...] = nt(read_ref[...], write0).astype(BF16)
    cum3[...] = jnp.concatenate(split3(cum_ref[...]), axis=1)
    prior3[...] = jnp.concatenate(split3(jnp.broadcast_to(tot[0:1, 0:HEADS], (16, HEADS))), axis=1)
    cf3_buf[...] = jnp.concatenate(split3(cumf), axis=1)
    dtf3_buf[...] = jnp.concatenate(split3(dt), axis=1)
    r0_buf[...] = read0
    rowpos = my * SPAN + k * CHUNK + lax.broadcasted_iota(I32, (CHUNK, 128), 0)
    valid = (rowpos < length).astype(F32)
    head3 = rowpos < 3
    valid0 = (lax.broadcasted_iota(I32, (16, 128), 0) < length).astype(F32)

    def pair_body(i, total):
        l0 = pl.multiple_of(i * 128, 128)
        lanes = pl.ds(l0, 128)
        sel = pick_matrix(192, i)
        read = read_ref[...]
        e = jnp.exp2(nn(cum3[...], sel))
        cf = nn(cf3_buf[...], sel)
        dtf = nn(dtf3_buf[...], sel)
        x0 = jnp.concatenate([wfirst[:, lanes], f_in[:, lanes]], axis=0).astype(F32)
        v0 = conv_tile(x0, conv_w[:, lanes], conv_b[0:1, lanes], 16)
        v0f = v0.astype(F32)
        vd = v0f * dtf
        scaled = (jnp.exp2(cf[2:3] - cf) * vd).astype(BF16)
        owner = i // 8
        row = pl.multiple_of((i % 8) // 4 * HALF + (i % 4) * 128, 16)
        s0 = s0_all[owner, pl.ds(row, 128), :]
        prior = jnp.exp2(nn(prior3[...], sel)[0:1])
        a = (nt(read, s0) * jnp.exp2(cf[2:3]) + nn(rw_buf[...], scaled)) * prior + nn(read, pre_tile(i))
        lane = lax.broadcasted_iota(I32, (1, 128), 1)
        skip_lane = jnp.where(lane < 64, skip[2 * i], skip[2 * i + 1])
        y = y_ref[:, lanes].astype(F32) + e * a
        y0 = nt(r0_buf[...], s0) * jnp.exp2(cf) + skip_lane * v0f
        row16 = lax.broadcasted_iota(I32, (16, 128), 0)
        for s in range(3):
            term = sc0_buf[:, s : s + 1] * jnp.exp2(jnp.minimum(cf - cf[s : s + 1], 0.0)) * vd[s : s + 1]
            y0 = y0 + jnp.where(row16 >= s, term, 0.0)
        y0 = jnp.concatenate([y0, jnp.zeros((CHUNK - 16, 128), F32)], axis=0)
        y = jnp.where(head3, y0, y) * valid
        g = gate[:, lanes].astype(F32)
        v = y.astype(BF16).astype(F32) * silu(g)
        gated[:, lanes] = v
        return total + v * v

    def pre_tile(i):
        return pre[:, pl.ds(pl.multiple_of(i * 128, 128), 128)]

    total = lax.fori_loop(0, PAIRS, pair_body, jnp.zeros((CHUNK, 128), F32))
    scale = lax.rsqrt(jnp.sum(total, axis=1, keepdims=True) * (1.0 / INNER) + EPSILON)

    def norm_body(i, carry):
        lanes = pl.ds(pl.multiple_of(i * 128, 128), 128)
        out[:, lanes] = (gated[:, lanes] * scale * norm_w[0:1, lanes]).astype(BF16)
        return carry

    lax.fori_loop(0, PAIRS, norm_body, 0)


def mixer(lens, skip, y, gate, read, cum, pre, s0_all, tot, f_in, f_st, f_dt, wfirst, wfst,
          conv_w, conv_b, step_b, decay, norm_w):
    rows = lambda lanes: pl.BlockSpec((CHUNK, lanes), lambda k: (k, 0))
    return pl.pallas_call(
        mixer_kernel,
        grid=(CHUNKS,),
        out_shape=jax.ShapeDtypeStruct((SPAN, INNER), BF16),
        in_specs=[SM, SM, rows(INNER), rows(INNER), rows(128), rows(HEADS)] + [VM] * 13,
        out_specs=rows(INNER),
        scratch_shapes=[
            pltpu.VMEM((CHUNK, INNER), F32),
            pltpu.VMEM((16, 128), BF16),
            pltpu.VMEM((CHUNK, 192), BF16),
            pltpu.VMEM((CHUNK, 16), BF16),
            pltpu.VMEM((16, 16), F32),
            pltpu.VMEM((16, 192), BF16),
            pltpu.VMEM((16, 192), BF16),
            pltpu.VMEM((16, 192), BF16),
        ],
        compiler_params=pltpu.CompilerParams(vmem_limit_bytes=48 * 1024 * 1024),
        name="mixer",
    )(lens, skip, y, gate, read, cum, pre, s0_all, tot, f_in, f_st, f_dt, wfirst, wfst,
      conv_w, conv_b, step_b, decay, norm_w)


def place_kernel(a, b, fin, whole, states):
    j = pl.program_id(0)
    states[0, 0:512, :] = a[0, 0:512, :].astype(F32)
    states[0, 512:1024, :] = b[0, 0:512, :].astype(F32)

    @pl.when(j == 0)
    def _():
        states[0] = states[0] * whole[...] + fin[...]


def place(out_a, out_b, fin, whole):
    half = pl.BlockSpec((1, HALF, 128), lambda j: (j, 0, 0))
    return pl.pallas_call(
        place_kernel,
        grid=(SLOTS,),
        out_shape=jax.ShapeDtypeStruct((SLOTS, 1024, 128), F32),
        in_specs=[half, half, VM, VM],
        out_specs=pl.BlockSpec((1, 1024, 128), lambda j: (j, 0, 0)),
        name="place",
    )(out_a, out_b, fin, whole)


def on_device(
    pool_states, inner_window, state_window, move_plan, active_mask, inputs_inner, inputs_state, gate_rows,
    step_raw, lengths, conv_weight, conv_bias, step_bias, decay_log, skip_weight, norm_weight,
):
    my = lax.axis_index("seq")
    match = (move_plan[None, :, 0] == jnp.arange(32, dtype=I32)[:, None]).astype(I32)
    slot = jnp.sum(match * jnp.arange(SLOTS, dtype=I32)[None, :], axis=1)
    keep = jnp.sum(match * active_mask[None, :], axis=1)
    tag = jnp.sum(match * (move_plan[None, :, 1] + 1), axis=1)
    meta = jnp.stack([slot, keep], axis=1)
    tags = jnp.broadcast_to(tag[:, None, None], (32, 1, 128))
    win = jnp.concatenate(
        [
            inner_window.reshape(SLOTS, 24, 128),
            jnp.pad(state_window.reshape(SLOTS, 192), ((0, 0), (0, 64))).reshape(SLOTS, 2, 128),
            jnp.zeros((SLOTS, 6, 128), BF16),
        ],
        axis=1,
    )
    conv_b = conv_bias[None]
    step_b = step_bias[None]
    decay = decay_log[None]
    (out_a, out_b, s0_all, f_in, f_st, f_dt, y, read, cum, pre, tot, fin, kept) = exchange(
        meta, lengths, skip_weight, tags, pool_states.reshape(SLOTS, 1024, 128), win,
        inputs_inner[0], inputs_state[0], step_raw[0], conv_weight, conv_b, step_b, decay,
    )
    tail = jnp.concatenate([s0_all[:, 0, 512:528], s0_all[:, 1, 512:528]], axis=1)
    w_in = jnp.moveaxis(tail[:, 0:24].reshape(4, 3, 1024), 0, 1).reshape(3, INNER)
    w_st = jnp.moveaxis(tail[:, 24:26].reshape(4, 256)[:, :192].reshape(4, 3, 64), 0, 1).reshape(3, 256)
    wfirst = jnp.concatenate([jnp.zeros((13, INNER), BF16), w_in], axis=0)
    wfst = jnp.concatenate([jnp.zeros((13, 256), BF16), w_st], axis=0)
    mixer_out = mixer(
        lengths, skip_weight, y, gate_rows[0], read, cum, pre, s0_all.reshape(4, 2 * HALF, 128), tot, f_in, f_st, f_dt,
        wfirst, wfst, conv_weight, conv_b, step_b, decay, norm_weight[None],
    )[None]
    live = (jnp.arange(3) < lengths[0]).astype(F32)[:, None]
    dt = jax.nn.softplus(f_dt[:3].astype(F32) + step_bias) * live
    rate = dt * -jnp.exp(decay_log)
    cumf = jnp.cumsum(rate, axis=0)
    ext_in = jnp.concatenate([w_in, f_in[:3]], axis=0).astype(F32)
    ext_st = jnp.concatenate([w_st, f_st[:3]], axis=0).astype(F32)
    own_in = lax.dynamic_slice_in_dim(ext_in, my * 1024, 1024, 1)
    own_w = lax.dynamic_slice_in_dim(conv_weight, my * 1024, 1024, 1)
    own_b = lax.dynamic_slice_in_dim(conv_bias, my * 1024, 1024, 0)
    v0 = own_b + sum(own_w[k] * own_in[k : k + 3] for k in range(4))
    v0 = jax.nn.silu(v0).astype(BF16).astype(F32)
    w0 = conv_bias[INNER : INNER + 128] + sum(
        conv_weight[k, INNER : INNER + 128] * ext_st[k : k + 3, 0:128] for k in range(4)
    )
    w0 = jax.nn.silu(w0).astype(BF16).astype(F32)
    left = jnp.exp(cumf[2:3] - cumf) * dt * jnp.exp2(tot[1:2, 0:HEADS])
    left = lax.dynamic_slice_in_dim(left, my * 16, 16, 1)
    whole = jnp.exp(cumf[2]) * jnp.exp2(tot[1, 0:HEADS])
    whole = lax.dynamic_slice_in_dim(whole, my * 16, 16, 0)
    sc3 = (left[:, :, None] * v0.reshape(3, 16, 64)).reshape(3, 1024)
    fin = fin + jnp.sum(sc3[:, :, None] * w0[:, None, :], axis=0)
    whole = jnp.broadcast_to(whole[:, None, None], (16, 64, 128)).reshape(1024, 128)
    new_states = place(out_a, out_b, fin, whole).reshape(SLOTS, 16, 64, 128)
    new_in = jnp.concatenate([out_a[:, 512:528], out_b[:, 512:520]], axis=1).reshape(SLOTS, 3, 1024)
    new_st = out_b[:, 520:522].reshape(SLOTS, 256)[:, :192].reshape(SLOTS, 3, 64)
    kept_in = kept[None, 0:3, 0:1024]
    kept_st = lax.dynamic_slice_in_dim(kept[3:6, 1024:1280], my * 64, 64, 1)[None]
    new_in = jnp.concatenate([kept_in, new_in[1:]], axis=0)
    new_st = jnp.concatenate([kept_st, new_st[1:]], axis=0)
    return (new_states, new_in, new_st, mixer_out)


def solution(mesh):
    return jax.shard_map(
        on_device,
        mesh=mesh,
        in_specs=(
            P("req", "seq", None, None), P("req", None, "seq"), P("req", None, "seq"), P("req", None), P("req"),
            P("req", "seq", None), P("req", "seq", None), P("req", "seq", None), P("req", "seq", None), P("req"),
            P(), P(), P(), P(), P(), P(),
        ),
        out_specs=(
            P("req", "seq", None, None), P("req", None, "seq"), P("req", None, "seq"), P("req", "seq", None),
        ),
        check_vma=False,
    )
```

time: 448 us -> 244 us (0.54)
  Pallas kernels: 0 us -> 204 us
  waiting for transfers between devices: 138 us -> 0 us
  other arithmetic: 96.7 us -> 6.61 us
  local copies, waits for them, and re-layouts: 102 us -> 29 us
  starting transfers between devices: 40.1 us -> 0 us
  matrix products: 27.7 us -> 0 us
  blocking collectives: 25.9 us -> 0 us
  between operations: 15.9 us -> 1.45 us
    pallas_call x0 -> x3, Pallas kernels: none -> 204 us  [the longest x1 142 us: exchange(): pl.pallas_call(exchange_kernel, out_shape=out_shape, in_specs=[SM, SM, SM...]
    all_to_all x4 -> x0, waiting for transfers between devices: 112 us -> none  [the longest x1 105 us: migrate(): lax.all_to_all(send_states.astype(jnp.bfloat16), 'req', split_axis=0, con...]
    all_to_all x4 -> x0, starting transfers between devices: 36.4 us -> none  [the longest x1 13.4 us: migrate(): lax.all_to_all(send_states.astype(jnp.bfloat16), 'req', split_axis=0, con...]
    reshape x3 -> x6, local copies, waits for them, and re-layouts: 31.1 us -> 0.38 us  [the longest x1 0.1 us: on_device(): state_window.reshape(SLOTS, 192)]
    dot_general x8 -> x0, matrix products: 27.7 us -> none  [the longest x2 15.6 us: block_local(): jnp.einsum('hts,shp->thp', weights, value_rows, preferred_element_type=jn...]
    all_gather x2 -> x0, waiting for transfers between devices: 25.6 us -> none  [the longest x1 25.6 us: on_device(): lax.all_gather(moved_states[:PREFILLS], 'seq', axis=1, tiled=True)]
    convert_element_type x12 -> x4, other arithmetic: 24.3 us -> 0.11 us  [the longest x1 0.09 us: on_device(): ext_in = jnp.concatenate([w_in, f_in[:3]], axis=0).astype(F32)]
    gather x9 -> x0, local copies, waits for them, and re-layouts: 19.8 us -> none  [the longest x3 11 us: placed(): return jnp.take(source.reshape((-1,) + source.shape[2:]), chosen, axis=0)]
  transfers between devices with their start and end apart: 10 -> 0, of which waited for: 3 -> 0; matrix products, arithmetic and copies ran while one was open for 34% -> 0% of each run, Pallas kernels for 0% -> 0%
where the time goes in v1:
time: 244 us; the launch traced here: 241 us
  Pallas kernels  204 us (84%)
  local copies, waits for them, and re-layouts  29 us (12%)
  other arithmetic  6.61 us (3%)
    pallas_call x1, Pallas kernels, exchange(): pl.pallas_call(exchange_kernel, out_shape=out_shape, in_specs=[SM, SM, SM...  142 us
    pallas_call x1, Pallas kernels, mixer(): pl.pallas_call(mixer_kernel, grid=(CHUNKS,), out_shape=jax.ShapeDtypeStru...  51.7 us
    unnamed x42, local copies, waits for them, and re-layouts  15.5 us
    pallas_call x1, Pallas kernels, place(): pl.pallas_call(place_kernel, grid=(SLOTS,), out_shape=jax.ShapeDtypeStruc...  9.76 us

profile of v1, /device:TPU:1, one launch (start us, length us, event | category | flops | bytes accessed | tf_op | source)
XLA Modules:
  0.0 240.8 jit_solution(230829558665255804)
XLA Ops:
  0.6 0.8 slice_bitcast_fusion.9
  1.4 0.7 select_reduce_fusion
  2.2 0.7 copy.50.meta
  2.8 0.7 broadcast_in_dim.24.tags
  4.2 1.3 broadcast_in_dim.26.conv_b
  5.5 1.0 copy.47
  6.6 0.7 copy.48
  7.3 0.1 reshape.89
  7.5 0.7 maximum_maximum_fusion.win
  8.2 1.6 copy.49
  9.8 142.3 %exchange.1 = (bf16[13,528,128]{2,1,0:T(8,128)(2,1)}, bf16[13,528,128]{2,1,0:T(8,128)(2,1)}, bf16[4,2,528,128]{3,2,1,0:T(8,128)(2,1)}, bf16[16,4096]{1,0:T(8,128...) custom-call(s32[32,2]{1,0:T(8,128)} %copy.50.meta, ...), custom_call_target="tpu_custom_call" | custom-call | tf_op jit(solution)/shard_map/exchange/pallas_call | solution.py:468
  152.2 0.7 slice_bitcast_fusion.1
  152.9 0.7 slice_bitcast_fusion
  153.9 1.2 copy-done
  155.1 1.2 copy-done.1
  156.4 0.9 copy-done.2
  157.2 0.9 copy-done.3
  158.2 0.9 copy-done.4
  159.1 0.7 copy-done.5
  159.8 0.9 copy-done.6
  160.7 0.7 copy-done.7
  161.4 0.7 copy-done.8
  162.1 0.7 copy-done.9
  162.8 0.7 copy-done.10
  163.5 0.7 copy-done.12
  164.1 0.7 copy-done.13
  164.8 0.7 copy-done.14
  165.5 51.7 %mixer.1 = bf16[512,4096]{1,0:T(8,128)(2,1)} custom-call(s32[1]{0:T(128)} %copy.62.lens, f32[64]{0:T(128)S(1)} %copy-done.13, bf16[512,4096]{1,0:T(8,128)(2,1)} %get-tuple-element.26.y_ref, bf16[512,4096]{1,0:T(8,128)(2,1)} %bitcast.68, bf16[512,128]{1,0:T(8,128)(2,1)S(1)} %copy-done.6, f32[512,64]{1,0:T(8,128)S(1)} %copy-done.3, ...), custom_call_target="tpu_custom_call" | custom-call | tf_op jit(solution)/shard_map/mixer/pallas_call | solution.py:563
  217.3 0.7 exponential_bitcast_fusion
  218.0 0.7 multiply_multiply_fusion
  218.8 0.1 mul.197
  218.9 0.9 slice.127
  219.8 0.1 fusion.1
  219.9 0.9 constant_dynamic-slice_fusion
  221.0 0.7 slice.139
  221.7 0.8 slice_bitcast_fusion.7
  222.5 0.5 multiply_reduce_fusion
  223.0 0.8 add.108.fin
  223.9 0.7 exponential_multiply_fusion
  224.8 1.0 broadcast_in_dim.59.whole
  225.8 9.8 %place.1 = f32[13,1024,128]{2,1,0:T(8,128)} custom-call(bf16[13,528,128]{2,1,0:T(8,128)(2,1)} %get-tuple-element.17.a, bf16[13,528,128]{2,1,0:T(8,128)(2,1)} %get-tuple-element.18.b, f32[1024,128]{1,0:T(8,128)} %add.108.fin, f32[1024,128]{1,0:T(8,128)} %broadcast_in_dim.59.whole), custom_call_target="tpu_custom_call" | custom-call | tf_op jit(solution)/shard_map/place/pallas_call | solution.py:597
  235.5 0.7 slice.149
  236.3 0.8 slice.148
  237.2 0.7 slice_bitcast_fusion.2
  237.9 0.7 pad_maximum_fusion
  238.6 0.7 slice.152
  239.3 0.7 slice.153
  240.2 0.6 copy.55
  (60 shorter events, 1.4 us)
Async XLA Ops:
  153.9 1.2 copy-start
  155.1 1.2 copy-start.1
  156.3 0.9 copy-start.2
  157.2 0.9 copy-start.3
  158.2 0.9 copy-start.4
  159.1 0.7 copy-start.5
  159.8 0.9 copy-start.6
  160.7 0.7 copy-start.7
  161.4 0.7 copy-start.8
  162.1 0.7 copy-start.9
  162.8 0.7 copy-start.10
  163.5 0.7 copy-start.12
  164.1 0.7 copy-start.13
  164.8 0.7 copy-start.14
  165.5 52.5 %copy-start.11 = (f32[64]{0:T(128)S(1)}, f32[64]{0:T(128)}, u32[]{:S(2)}) copy-start(f32[64]{0:T(128)} %param.28) | copy-start | bytes 772
  165.5 55.4 %copy-start.16 = (f32[4352]{0:T(1024)S(1)}, f32[4352]{0:T(1024)}, u32[]{:S(2)}) copy-start(f32[4352]{0:T(1024)} %param.27) | copy-start | bytes 52228
  165.5 57.0 %slice-start = ((f32[4352]{0:T(1024)}), f32[128]{0:T(128)S(1)}, s32[]{:S(2)}) async-start(f32[4352]{0:T(1024)} %param.27), calls=%async_computation | async-start | bytes 1024 | tf_op jit(solution)/shard_map/slice | solution.py:653
  165.5 57.5 %copy-start.15 = (f32[1024,128]{1,0:T(8,128)S(1)}, f32[1024,128]{1,0:T(8,128)}, u32[]{:S(2)}) copy-start(f32[1024,128]{1,0:T(8,128)} %get-tuple-element.19) | copy-start | bytes 1572868

commit v2 on v1

v2 whole, which is shorter than its diff:
```python
import functools

import jax
import jax.numpy as jnp
from jax import lax
from jax.experimental import pallas as pl
from jax.experimental.pallas import tpu as pltpu
from jax.sharding import PartitionSpec as P

MESH = pl.DeviceIdType.MESH
ANY = pl.BlockSpec(memory_space=pl.ANY)
VM = pl.BlockSpec(memory_space=pltpu.VMEM)
SM = pl.BlockSpec(memory_space=pltpu.SMEM)
F32 = jnp.float32
BF16 = jnp.bfloat16
I32 = jnp.int32

SLOTS = 13
HEADS = 64
INNER = 4096
SPAN = 512
CHUNK = 128
CHUNKS = SPAN // CHUNK
PAIRS = HEADS // 2
HALF = 528
GROUP = 2
LOG2E = 1.4426950408889634
EPSILON = 1e-05


def nn(a, b):
    return lax.dot_general(a, b, (((1,), (0,)), ((), ())), preferred_element_type=F32)


def nt(a, b):
    return lax.dot_general(a, b, (((1,), (1,)), ((), ())), preferred_element_type=F32)


def split3(v):
    hi = v.astype(BF16)
    rest = v - hi.astype(F32)
    mid = rest.astype(BF16)
    lo = (rest - mid.astype(F32)).astype(BF16)
    return hi, mid, lo


def silu(v):
    half = 0.5 * v
    return half + half * jnp.tanh(half)


def softplus(v):
    u = jnp.exp(-jnp.abs(v))
    series = u * (1.0 - u * (0.5 - u * (1.0 / 3.0 - u * (0.25 - u * 0.2))))
    return jnp.maximum(v, 0.0) + jnp.where(u < 0.02, series, jnp.log(1.0 + u))


def pick_lanes(copies, pair):
    row = lax.broadcasted_iota(I32, (64, 128), 0)
    lane = lax.broadcasted_iota(I32, (64, 128), 1)
    one = jnp.where(row == 2 * pair + (lane >= 64).astype(I32), 1.0, 0.0).astype(BF16)
    return jnp.concatenate([one] * copies, axis=0)


def pick_heads(copies, pair):
    row = lax.broadcasted_iota(I32, (64, 256), 0)
    lane = lax.broadcasted_iota(I32, (64, 256), 1)
    one = jnp.where(row == 2 * pair + (lane >= 128).astype(I32), 1.0, 0.0).astype(BF16)
    return jnp.concatenate([one] * copies, axis=0)


def conv_tile(x, taps, bias, rows):
    acc = bias + taps[3:4] * x[16 : 16 + rows]
    for k in range(3):
        acc = acc + taps[k : k + 1] * x[13 + k : 13 + k + rows]
    return silu(acc).astype(BF16)


def exchange_kernel(
    meta, lens, skip, tags, tags_b, pool, win, xin, xst, gate, step, conv_w, conv_b, step_b, decay, norm_w,
    moved, wout, fin_out, mix,
    stage, sbuf_a, sbuf_b, rel_a, rel_b, near_a, near_b, far_a, far_b, xbuf, xsbuf, gbuf, y_buf, read_buf, cum_buf, st_buf,
    lsend, lrecv, ssend, srecv, tbuf, tagbuf, rtag_a, rtag_b, tag_s, rtag_as, rtag_bs,
    cum3, cumt, dt2, sc_buf, wt_buf, base_buf, wtile, fin_buf, wstage, ffin, ffst, ffdt,
    small3, w0t, read0_buf, sc0_buf,
    pool_sem, in_sem, out_sem, one_send, one_recv, two_send, two_recv, tag_send, tag_recv, rt_send, rt_recv,
    halo_send, halo_recv, lend_send, lend_recv, win_send, win_recv, s0_send, s0_recv, f_send, f_recv,
):
    me = lax.axis_index("req")
    my = lax.axis_index("seq")
    mx, mz, mc = me // 8, (me // 2) % 4, me % 2

    def at(dx, dz, dc):
        return ((mx + dx) % 4) * 8 + ((mz + dz) % 4) * 2 + (mc + dc) % 2

    loads = []
    for k in range(SLOTS):
        cp = pltpu.make_async_copy(pool.at[k], stage.at[k], pool_sem.at[k])
        cp.start()
        loads.append(cp)
    ins = [
        pltpu.make_async_copy(xin, xbuf.at[pl.ds(16, SPAN)], in_sem.at[0]),
        pltpu.make_async_copy(xst, xsbuf.at[pl.ds(16, SPAN)], in_sem.at[1]),
    ]
    for cp in ins:
        cp.start()
    gate_load = pltpu.make_async_copy(gate, gbuf, in_sem.at[2])
    gate_load.start()

    barrier = pltpu.get_barrier_semaphore()
    for r in range(1, 32):
        peer = at(r // 8, (r // 2) % 4, r % 2)
        pl.semaphore_signal(barrier, inc=1, device_id=(peer, my), device_id_type=MESH)
    for r in range(1, 4):
        pl.semaphore_signal(barrier, inc=1, device_id=(me, (my + r) % 4), device_id_type=MESH)
    pl.semaphore_wait(barrier, 34)

    def send(src, dst, ssem, rsem, dev):
        cp = pltpu.make_async_remote_copy(
            src_ref=src, dst_ref=dst, send_sem=ssem, recv_sem=rsem, device_id=dev, device_id_type=MESH
        )
        cp.start()
        return cp

    halo = [
        send(xin.at[pl.ds(SPAN - 16, 16)], xbuf.at[pl.ds(0, 16)], halo_send.at[0], halo_recv.at[0], (me, (my + 1) % 4)),
        send(xst.at[pl.ds(SPAN - 16, 16)], xsbuf.at[pl.ds(0, 16)], halo_send.at[1], halo_recv.at[1], (me, (my + 1) % 4)),
    ]
    firsts = []
    for r in range(1, 4):
        dev = (me, (my + r) % 4)
        firsts.append(send(xin.at[pl.ds(0, 16)], ffin.at[my], f_send.at[r], f_recv.at[r], dev))
        firsts.append(send(xst.at[pl.ds(0, 16)], ffst.at[my], f_send.at[4 + r], f_recv.at[4 + r], dev))
        firsts.append(send(step.at[pl.ds(0, 16)], ffdt.at[my], f_send.at[8 + r], f_recv.at[8 + r], dev))

    for cp in loads:
        cp.wait()

    def fill(ref, lead, q, dest, half):
        slot = meta[dest, 0]
        keep = meta[dest, 1].astype(F32)
        ref[lead, q, pl.ds(0, 512), :] = (stage[slot, pl.ds(512 * half, 512), :] * keep).astype(BF16)
        ref[lead, q, pl.ds(512, 16), :] = (win[slot, pl.ds(16 * half, 16), :].astype(F32) * keep).astype(BF16)

    def fill_a(ref, lead, xd):
        def one(q, carry):
            fill(ref, lead, q, xd * 8 + q, 0)
            return carry

        lax.fori_loop(0, 8, one, 0)

    def fill_b(ref, lead, zd):
        def one(q, carry):
            fill(ref, lead, q, (q // 2) * 8 + zd * 2 + q % 2, 1)
            return carry

        lax.fori_loop(0, 8, one, 0)

    phase_a, phase_b, rtags = {}, {}, []
    for d in (2, 1, 3):
        xd, zd = (mx + d) % 4, (mz + d) % 4
        dev_a, dev_b = (at(d, 0, 0), my), (at(0, d, 0), my)
        fill_a(sbuf_a, xd, xd)
        phase_a[d] = send(sbuf_a.at[xd], rel_a.at[mx], one_send.at[d], one_recv.at[d], dev_a)
        fill_b(sbuf_b, zd, zd)
        phase_b[d] = send(sbuf_b.at[zd], rel_b.at[mz], one_send.at[4 + d], one_recv.at[4 + d], dev_b)
        rtags.append(send(tags.at[pl.ds(xd * 8, 8)], rtag_a.at[mx], rt_send.at[d], rt_recv.at[d], dev_a))
        rtags.append(send(tags_b.at[zd], rtag_b.at[mz], rt_send.at[4 + d], rt_recv.at[4 + d], dev_b))
    fill_a(rel_a, mx, mx)
    fill_b(rel_b, mz, mz)

    second = {}

    def row_a(p):
        return (near_a if p < 2 else far_a).at[(p % 2) * 8 + mz * 2 + mc]

    def row_b(p):
        return (near_b if p < 2 else far_b).at[(p % 2) * 8 + mx * 2 + mc]

    def forward(p, e, src_a, src_b):
        de, dc = e // 2, e % 2
        sem = p * 8 + e
        second[p, e, 0] = send(
            src_a, row_a(p), two_send.at[sem], two_recv.at[sem], (at(0, de, dc), my))
        second[p, e, 1] = send(
            src_b, row_b(p), two_send.at[32 + sem], two_recv.at[32 + sem], (at(de, 0, dc), my))

    def targets(e):
        de, dc = e // 2, e % 2
        ct = (mc + dc) % 2
        return ((mz + de) % 4) * 2 + ct, ((mx + de) % 4) * 2 + ct

    for e in range(1, 8):
        ta, tb = targets(e)
        forward(0, e, rel_a.at[mx, ta], rel_b.at[mz, tb])
    row_a(0)[...] = rel_a[mx, mz * 2 + mc]
    row_b(0)[...] = rel_b[mz, mx * 2 + mc]

    tag_copies = []
    for r in range(1, 32):
        peer = at(r // 8, (r // 2) % 4, r % 2)
        tag_copies.append(
            send(tags.at[peer], tagbuf.at[me], tag_send.at[r], tag_recv.at[r], (peer, my))
        )
    tagbuf[me] = tags[me]

    for cp in ins:
        cp.wait()
    for cp in halo:
        cp.wait()

    @pl.when(my == 0)
    def _():
        xbuf[pl.ds(0, 16), :] = jnp.zeros((16, INNER), BF16)
        xsbuf[pl.ds(0, 16), :] = jnp.zeros((16, 256), BF16)

    st_buf[...] = jnp.zeros_like(st_buf)
    base_buf[...] = jnp.zeros_like(base_buf)
    length = lens[0]

    def chunk_body(k, carry):
        r0 = pl.multiple_of(k * CHUNK, CHUNK)
        pos = my * SPAN + r0 + lax.broadcasted_iota(I32, (CHUNK, HEADS), 0)
        live = ((pos < length) & (pos >= 3)).astype(F32)
        dt = softplus(step[pl.ds(r0, CHUNK), :].astype(F32) + step_b[0:1, :]) * live
        rate = dt * (-LOG2E * jnp.exp(decay[0:1, :]))
        rows = lax.broadcasted_iota(I32, (CHUNK, CHUNK), 0)
        cols = lax.broadcasted_iota(I32, (CHUNK, CHUNK), 1)
        tri = jnp.where(rows >= cols, 1.0, 0.0).astype(BF16)
        hi, mid, lo = split3(rate)
        cum = nn(tri, hi) + nn(tri, mid) + nn(tri, lo)
        cum3[...] = jnp.concatenate(split3(cum), axis=1)
        cumt[...] = jnp.transpose(cum)
        dth = dt.astype(BF16)
        dt2[...] = jnp.concatenate([dth, (dt - dth.astype(F32)).astype(BF16)], axis=1)
        cum_buf[pl.ds(r0, CHUNK), :] = cum + base_buf[0:1, 0:HEADS]
        base_buf[0:1, 0:HEADS] = base_buf[0:1, 0:HEADS] + cum[CHUNK - 1 : CHUNK, :]
        xs_tile = xsbuf[pl.ds(r0, CHUNK + 16), :].astype(F32)
        mixed = conv_tile(xs_tile, conv_w[:, INNER : INNER + 256], conv_b[0:1, INNER : INNER + 256], CHUNK)
        write, read = mixed[:, 0:128], mixed[:, 128:256]
        read_buf[pl.ds(r0, CHUNK), :] = read
        sc_buf[...] = jnp.where(rows >= cols, nt(read, write), 0.0)
        wt_buf[...] = jnp.transpose(write.astype(F32)).astype(BF16)

        def group_body(j, inner):
            lanes = [pl.ds(pl.multiple_of(j * (GROUP * 128) + g * 128, 128), 128) for g in range(GROUP)]
            pairs = [j * GROUP + g for g in range(GROUP)]
            every = range(GROUP)
            low = lax.broadcasted_iota(I32, (CHUNK, 128), 1) < 64
            lane = lax.broadcasted_iota(I32, (1, 128), 1)
            x = [xbuf[pl.ds(r0, CHUNK + 16), lanes[g]].astype(F32) for g in every]
            state = [st_buf[:, lanes[g]] for g in every]
            both = [nn(cum3[...], pick_heads(3, pairs[g])) for g in every]
            dte = [nn(dt2[...], pick_lanes(2, pairs[g])) for g in every]
            carried = [nn(read_buf[pl.ds(r0, CHUNK), :], state[g].astype(BF16)) for g in every]
            value = [conv_tile(x[g], conv_w[:, lanes[g]], conv_b[0:1, lanes[g]], CHUNK).astype(F32) for g in every]
            ys, states = [], []
            for g in every:
                sc = sc_buf[...]
                c1, c2 = both[g][:, 0:128], both[g][:, 128:256]
                w1 = sc * jnp.exp2(jnp.minimum(c1 - cumt[pl.ds(2 * pairs[g], 1), :], 0.0))
                w2 = sc * jnp.exp2(jnp.minimum(c2 - cumt[pl.ds(2 * pairs[g] + 1, 1), :], 0.0))
                cp = jnp.where(low, c1, c2)
                vd = value[g] * dte[g]
                zero = jnp.zeros_like(vd)
                rhs = jnp.concatenate([jnp.where(low, vd, zero), jnp.where(low, zero, vd)], axis=0).astype(BF16)
                lhs = jnp.concatenate([w1.astype(BF16), w2.astype(BF16)], axis=1)
                last = cp[CHUNK - 1 : CHUNK, :]
                scaled = (jnp.exp2(last - cp) * vd).astype(BF16)
                skip_lane = jnp.where(lane < 64, skip[2 * pairs[g]], skip[2 * pairs[g] + 1])
                ys.append(nn(lhs, rhs) + carried[g] * jnp.exp2(cp) + skip_lane * value[g])
                states.append(jnp.exp2(last) * state[g] + nn(wt_buf[...], scaled))
            for g in every:
                y_buf[pl.ds(r0, CHUNK), lanes[g]] = ys[g].astype(BF16)
                st_buf[:, lanes[g]] = states[g]
            return inner

        lax.fori_loop(0, PAIRS // GROUP, group_body, 0)
        return carry

    lax.fori_loop(0, CHUNKS, chunk_body, 0)

    cols = lax.broadcasted_iota(I32, (16, SPAN), 1)
    rows = lax.broadcasted_iota(I32, (16, SPAN), 0)
    want = length - 3 - my * SPAN
    sel_in = jnp.where((cols == want + rows) & (rows < 3), 1.0, 0.0).astype(BF16)
    sel_st = jnp.where((cols == want + rows - 3) & (rows >= 3) & (rows < 6), 1.0, 0.0).astype(BF16)
    small3[0:16, :] = jnp.zeros((16, 192), BF16)
    lst = nn(sel_st, xsbuf[pl.ds(16, SPAN), :])

    def lend_body(i, carry):
        lanes = pl.ds(pl.multiple_of(i * 256, 256), 256)
        to = pl.ds(pl.multiple_of((i % 4) * 256, 256), 256)
        lsend[i // 4, pl.ds(0, 128), to] = st_buf[:, lanes].astype(BF16)
        first = jnp.where(i % 4 == 0, 1.0, 0.0)
        lsend[i // 4, pl.ds(128, 16), to] = (nn(sel_in, xbuf[pl.ds(16, SPAN), lanes]) + first * lst).astype(BF16)
        return carry

    lax.fori_loop(0, INNER // 256, lend_body, 0)
    tbuf[my] = base_buf[...]
    lrecv[my] = lsend[my]
    lends = []
    for r in range(1, 4):
        dev = (me, (my + r) % 4)
        lends.append(send(lsend.at[(my + r) % 4], lrecv.at[my], lend_send.at[r], lend_recv.at[r], dev))
        lends.append(send(tbuf.at[my], tbuf.at[my], lend_send.at[4 + r], lend_recv.at[4 + r], dev))

    for cp in rtags:
        cp.wait()
    tag_loads = [
        pltpu.make_async_copy(rtag_a, rtag_as, in_sem.at[3]),
        pltpu.make_async_copy(rtag_b, rtag_bs, in_sem.at[4]),
    ]
    for cp in tag_loads:
        cp.start()
    for d in (1, 3, 2):
        phase_a[d].wait()
        phase_b[d].wait()
    for cp in tag_loads:
        cp.wait()

    def swapped(first, p):
        if p == 1:
            return jnp.where(first >= 2, first, 1)
        return jnp.where(first == p, 1, p)

    for p in (1, 2, 3):
        for e in range(8):
            ta, tb = targets(e)
            first_a, first_b = jnp.int32(0), jnp.int32(0)
            for q in (1, 2, 3):
                first_a = first_a + jnp.where(rtag_as[(mx + 4 - q) % 4, ta, 0, 0] == 1, q, 0)
                first_b = first_b + jnp.where(rtag_bs[(mz + 4 - q) % 4, tb, 0, 0] == 1, q, 0)
            block_a = rel_a[(mx + 4 - swapped(first_a, p)) % 4, ta]
            block_b = rel_b[(mz + 4 - swapped(first_b, p)) % 4, tb]
            if e == 0:
                row_a(p)[...] = block_a
                row_b(p)[...] = block_b
            else:
                sbuf_a[p, e] = block_a
                sbuf_b[p, e] = block_b
                forward(p, e, sbuf_a.at[p, e], sbuf_b.at[p, e])

    for cp in tag_copies:
        cp.wait()
    tag_load = pltpu.make_async_copy(tagbuf, tag_s, in_sem.at[5])
    tag_load.start()
    tag_load.wait()

    def source_of(j):
        acc = jnp.int32(0)
        for s in range(32):
            acc = acc + jnp.where(tag_s[s, 0, 0] == j + 1, s, 0)
        return acc

    def split_source(src):
        xs, zs, cs = src // 8, (src // 2) % 4, src % 2
        return (mx + 4 - xs) % 4, zs * 2 + cs, (mz + 4 - zs) % 4, xs * 2 + cs

    hops0_a, relay0_a, hops0_b, relay0_b = split_source(source_of(0))
    loc0_a = jnp.where(hops0_a > 0, 8, 0) + relay0_a
    loc0_b = jnp.where(hops0_b > 0, 8, 0) + relay0_b

    def rank(hops, relay, hops0, relay0):
        moved_up = jnp.where(hops == hops0, 1, jnp.where(hops == 1, hops0, hops))
        place_in = jnp.where((relay == relay0) & (hops0 >= 2) & (hops > 0), moved_up, hops)
        return place_in * 8 + relay

    def places(j):
        hops_a, relay_a, hops_b, relay_b = split_source(source_of(j))
        return rank(hops_a, relay_a, hops0_a, relay0_a), rank(hops_b, relay_b, hops0_b, relay0_b)

    def fetch(near, far, loc):
        return jnp.where(loc < 16, near[jnp.minimum(loc, 15)], far[jnp.maximum(loc - 16, 0)])

    for cp in firsts:
        cp.wait()
    own_first = [
        pltpu.make_async_copy(xin.at[pl.ds(0, 16)], ffin.at[my], in_sem.at[6]),
        pltpu.make_async_copy(xst.at[pl.ds(0, 16)], ffst.at[my], in_sem.at[7]),
    ]
    for cp in own_first:
        cp.start()
    ffdt[my] = step[pl.ds(0, 16), :]
    for cp in own_first:
        cp.wait()
    for cp in lends:
        cp.wait()

    for p in (0, 1):
        for e in range(1, 8):
            second[p, e, 0].wait()
            second[p, e, 1].wait()

    wtile[my] = near_b[loc0_b, pl.ds(512, 16), :]
    wins = []
    for r in range(1, 4):
        wins.append(send(wtile.at[my], wtile.at[my], win_send.at[r], win_recv.at[r], (me, (my + r) % 4)))

    posf = lax.broadcasted_iota(I32, (16, HEADS), 0)
    livef = ((posf < length) & (posf < 3)).astype(F32)
    dtf0 = softplus(ffdt[0].astype(F32) + step_b[0:1, :]) * livef
    rate0 = dtf0 * (-LOG2E * jnp.exp(decay[0:1, :]))
    c0 = rate0[0:1]
    c1 = c0 + rate0[1:2]
    c2 = c1 + rate0[2:3]
    cumf = jnp.where(posf == 0, c0, jnp.where(posf == 1, c1, c2))
    totals = jnp.where(posf == 0, tbuf[0][0:1, 0:HEADS], jnp.where(
        posf == 1, tbuf[1][0:1, 0:HEADS], jnp.where(posf == 2, tbuf[2][0:1, 0:HEADS], tbuf[3][0:1, 0:HEADS])))
    small3[0:16, :] = jnp.concatenate(split3(cumf), axis=1)
    small3[16:32, :] = jnp.concatenate(split3(dtf0), axis=1)
    small3[32:48, :] = jnp.concatenate(split3(totals), axis=1)

    for cp in wins:
        cp.wait()
    w_low = wtile[0].astype(F32) + wtile[1].astype(F32)
    w_high = wtile[2].astype(F32) + wtile[3].astype(F32)
    e_st = jnp.concatenate([jnp.concatenate([w_low, w_high], axis=1), ffst[0].astype(F32)], axis=0)
    mixed0 = conv_tile(e_st, conv_w[:, INNER : INNER + 256], conv_b[0:1, INNER : INNER + 256], 16)
    write0, read0 = mixed0[:, 0:128], mixed0[:, 128:256]
    read0_buf[...] = read0
    sc0_buf[...] = nt(read0, write0)
    w0t[...] = jnp.transpose(
        jnp.concatenate([write0.astype(F32), jnp.zeros((112, 128), F32)], axis=0)).astype(BF16)

    row16 = lax.broadcasted_iota(I32, (16, 128), 0)
    lane1 = lax.broadcasted_iota(I32, (1, 128), 1)
    for q in range(8):
        i = my * 8 + q
        lanes = pl.ds(pl.multiple_of(my * 1024 + q * 128, 128), 128)
        own = pl.ds(q * 128, 128)
        if q < 4:
            s0 = near_a[loc0_a, pl.ds(q * 128, 128), :]
        else:
            s0 = near_b[loc0_b, pl.ds((q - 4) * 128, 128), :]
        s0t = jnp.transpose(s0.astype(F32))
        wa = near_a[loc0_a, pl.ds(512, 16), :].astype(F32)
        wb = near_b[loc0_b, pl.ds(512, 16), :].astype(F32)
        wq = jnp.where(row16 == 13, wa[q : q + 1], jnp.where(row16 == 14, wa[8 + q : 9 + q], wb[q : q + 1]))
        x0 = jnp.concatenate([wq, ffin[0, :, lanes].astype(F32)], axis=0)
        small = nn(small3[...], pick_lanes(3, i))
        cf, dtf, totl = small[0:16], small[16:32], small[32:48]
        v0 = conv_tile(x0, conv_w[:, lanes], conv_b[0:1, lanes], 16).astype(F32)
        vd = v0 * dtf
        scaled = jnp.concatenate([jnp.exp2(cf[2:3] - cf) * vd, jnp.zeros((112, 128), F32)], axis=0).astype(BF16)
        carry = jnp.exp2(cf[2:3]) * s0t + nn(w0t[...], scaled)
        y0 = nt(read0_buf[...], s0) * jnp.exp2(cf)
        y0 = y0 + jnp.where(lane1 < 64, skip[2 * i], skip[2 * i + 1]) * v0
        for s in range(3):
            term = sc0_buf[:, s : s + 1] * jnp.exp2(jnp.minimum(cf - cf[s : s + 1], 0.0)) * vd[s : s + 1]
            y0 = y0 + jnp.where(row16 >= s, term, 0.0)
        kept = jnp.zeros((16, 128), F32)
        for c in range(4):
            ssend[c, pl.ds(0, 128), own] = carry.astype(BF16)
            ssend[c, pl.ds(128, 16), own] = y0.astype(BF16)
            carry = jnp.exp2(totl[c : c + 1]) * carry + lrecv[c, pl.ds(0, 128), own].astype(F32)
            kept = kept + lrecv[c, pl.ds(128, 16), own].astype(F32)
        fin_buf[pl.ds(q * 128, 128), :] = jnp.transpose(carry)
        for r in range(3):
            wstage[0, pl.ds(r * 8 + q, 1), :] = kept[r : r + 1]
        if q < 2:
            wstage[1 + q, pl.ds(0, 16), :] = kept

    sins = []
    for r in range(1, 4):
        other = (my + r) % 4
        sins.append(send(ssend.at[other], srecv.at[my], s0_send.at[r], s0_recv.at[r], (me, other)))
    srecv[my] = ssend[my]

    outs = []

    def put_out(src, dst, i):
        cp = pltpu.make_async_copy(src, dst, out_sem.at[i])
        cp.start()
        outs.append(cp)

    put_out(fin_buf, fin_out, 30)
    gate_load.wait()
    for cp in sins:
        cp.wait()

    @pl.when(my == 0)
    def _():
        rowc = lax.broadcasted_iota(I32, (16, HEADS), 0)
        cum_buf[pl.ds(0, 16), :] = jnp.where(rowc < 3, -1.0e6, cum_buf[pl.ds(0, 16), :])

        def patch(i, carry):
            lanes = pl.ds(pl.multiple_of(i * 256, 256), 256)
            new = srecv[i // 4, pl.ds(128, 16), pl.ds(pl.multiple_of((i % 4) * 256, 256), 256)].astype(F32)
            old = y_buf[pl.ds(0, 16), lanes].astype(F32)
            rowy = lax.broadcasted_iota(I32, (16, 256), 0)
            y_buf[pl.ds(0, 16), lanes] = jnp.where(rowy < 3, new, old).astype(BF16)
            return carry

        lax.fori_loop(0, INNER // 256, patch, 0)

    def tail_body(k, carry):
        r0 = pl.multiple_of(k * CHUNK, CHUNK)
        cum3[...] = jnp.concatenate(split3(cum_buf[pl.ds(r0, CHUNK), :]), axis=1)
        rowpos = my * SPAN + r0 + lax.broadcasted_iota(I32, (CHUNK, 128), 0)

        def group_body(j, total):
            lanes = [pl.ds(pl.multiple_of(j * 256 + g * 128, 128), 128) for g in range(2)]
            owner = j // 4
            valid = (rowpos < length).astype(F32)
            read = read_buf[pl.ds(r0, CHUNK), :]
            own = [pl.ds(pl.multiple_of((j % 4) * 256 + g * 128, 128), 128) for g in range(2)]
            ce = [nn(cum3[...], pick_lanes(3, 2 * j + g)) for g in range(2)]
            part = [nn(read, srecv[owner, pl.ds(0, 128), own[g]]) for g in range(2)]
            old = [y_buf[pl.ds(r0, CHUNK), lanes[g]].astype(F32) for g in range(2)]
            gates = [silu(gbuf[pl.ds(r0, CHUNK), lanes[g]].astype(F32)) for g in range(2)]
            new = []
            for g in range(2):
                y = (old[g] + jnp.exp2(ce[g]) * part[g]) * valid
                new.append(y.astype(BF16).astype(F32) * gates[g])
            for g in range(2):
                st_buf[:, lanes[g]] = new[g]
                total = total + new[g] * new[g]
            return total

        total = lax.fori_loop(0, PAIRS // 2, group_body, jnp.zeros((CHUNK, 128), F32))
        sc_buf[...] = jnp.broadcast_to(
            lax.rsqrt(jnp.sum(total, axis=1, keepdims=True) * (1.0 / INNER) + EPSILON), (CHUNK, CHUNK))

        def norm_body(i, inner):
            lanes = pl.ds(pl.multiple_of(i * 128, 128), 128)
            y_buf[pl.ds(r0, CHUNK), lanes] = (st_buf[:, lanes] * sc_buf[...] * norm_w[0:1, lanes]).astype(BF16)
            return inner

        lax.fori_loop(0, PAIRS, norm_body, 0)
        return carry

    lax.fori_loop(0, CHUNKS, tail_body, 0)
    put_out(y_buf, mix, 31)

    spots = [places(j) for j in range(SLOTS)]
    for p in (2, 3):
        for e in range(1, 8):
            second[p, e, 0].wait()
            second[p, e, 1].wait()
    for j in range(1, SLOTS):
        loc_a, loc_b = spots[j]
        sbuf_a[j // 8, j % 8] = fetch(near_a, far_a, loc_a)
        sbuf_b[j // 8, j % 8] = fetch(near_b, far_b, loc_b)
        put_out(sbuf_a.at[j // 8, j % 8, pl.ds(0, 512)], moved.at[j, pl.ds(0, 512)], 2 * j)
        put_out(sbuf_b.at[j // 8, j % 8, pl.ds(0, 512)], moved.at[j, pl.ds(512, 512)], 2 * j + 1)
        wstage[2 + j, pl.ds(0, 16), :] = sbuf_a[j // 8, j % 8, pl.ds(512, 16), :].astype(F32)
        wstage[2 + j, pl.ds(16, 16), :] = sbuf_b[j // 8, j % 8, pl.ds(512, 16), :].astype(F32)
    put_out(wstage, wout, 0)
    for cp in outs:
        cp.wait()


def exchange(meta, lens, skip, tags, tags_b, pool, win, xin, xst, gate, step, conv_w, conv_b, step_b, decay, norm_w):
    dma = pltpu.SemaphoreType.DMA
    shape = jax.ShapeDtypeStruct
    out_shape = (
        shape((SLOTS, 1024, 128), BF16),
        shape((SLOTS + 2, 32, 128), F32),
        shape((1024, 128), F32),
        shape((SPAN, INNER), BF16),
    )
    scratch = [
        pltpu.VMEM((SLOTS, 1024, 128), F32),
        pltpu.VMEM((4, 8, HALF, 128), BF16),
        pltpu.VMEM((4, 8, HALF, 128), BF16),
        pltpu.VMEM((4, 8, HALF, 128), BF16),
        pltpu.VMEM((4, 8, HALF, 128), BF16),
        pltpu.VMEM((16, HALF, 128), BF16),
        pltpu.VMEM((16, HALF, 128), BF16),
        pltpu.VMEM((16, HALF, 128), BF16),
        pltpu.VMEM((16, HALF, 128), BF16),
        pltpu.VMEM((SPAN + 16, INNER), BF16),
        pltpu.VMEM((SPAN + 16, 256), BF16),
        pltpu.VMEM((SPAN, INNER), BF16),
        pltpu.VMEM((SPAN, INNER), BF16),
        pltpu.VMEM((SPAN, 128), BF16),
        pltpu.VMEM((SPAN, HEADS), F32),
        pltpu.VMEM((128, INNER), F32),
        pltpu.VMEM((4, 144, 1024), BF16),
        pltpu.VMEM((4, 144, 1024), BF16),
        pltpu.VMEM((4, 144, 1024), BF16),
        pltpu.VMEM((4, 144, 1024), BF16),
        pltpu.VMEM((4, 8, 128), F32),
        pltpu.VMEM((32, 1, 128), I32),
        pltpu.VMEM((4, 8, 1, 128), I32),
        pltpu.VMEM((4, 8, 1, 128), I32),
        pltpu.SMEM((32, 1, 128), I32),
        pltpu.SMEM((4, 8, 1, 128), I32),
        pltpu.SMEM((4, 8, 1, 128), I32),
        pltpu.VMEM((CHUNK, 192), BF16),
        pltpu.VMEM((HEADS, CHUNK), F32),
        pltpu.VMEM((CHUNK, 128), BF16),
        pltpu.VMEM((CHUNK, CHUNK), F32),
        pltpu.VMEM((CHUNK, CHUNK), BF16),
        pltpu.VMEM((8, 128), F32),
        pltpu.VMEM((4, 16, 128), BF16),
        pltpu.VMEM((1024, 128), F32),
        pltpu.VMEM((SLOTS + 2, 32, 128), F32),
        pltpu.VMEM((4, 16, INNER), BF16),
        pltpu.VMEM((4, 16, 256), BF16),
        pltpu.VMEM((4, 16, HEADS), BF16),
        pltpu.VMEM((48, 192), BF16),
        pltpu.VMEM((128, 128), BF16),
        pltpu.VMEM((16, 128), BF16),
        pltpu.VMEM((16, 16), F32),
        dma((SLOTS,)), dma((8,)), dma((32,)),
        dma((8,)), dma((8,)), dma((64,)), dma((64,)), dma((32,)), dma((32,)), dma((8,)), dma((8,)),
        dma((2,)), dma((2,)), dma((8,)), dma((8,)), dma((4,)), dma((4,)), dma((4,)), dma((4,)), dma((12,)), dma((12,)),
    ]
    return pl.pallas_call(
        exchange_kernel,
        out_shape=out_shape,
        in_specs=[SM, SM, SM, VM, VM, ANY, VM, ANY, ANY, ANY, VM, VM, VM, VM, VM, VM],
        out_specs=[ANY] * len(out_shape),
        scratch_shapes=scratch,
        compiler_params=pltpu.CompilerParams(
            collective_id=1, has_side_effects=True, vmem_limit_bytes=67043328
        ),
        name="exchange",
    )(meta, lens, skip, tags, tags_b, pool, win, xin, xst, gate, step, conv_w, conv_b, step_b, decay, norm_w)


PLACE_ROWS = SLOTS * 256


def place_kernel(moved, fin, states):
    states[...] = moved[...].astype(F32)

    @pl.when(pl.program_id(0) == 0)
    def _():
        states[pl.ds(0, 1024), :] = fin[...]


def place(moved, fin):
    return pl.pallas_call(
        place_kernel,
        grid=(4,),
        out_shape=jax.ShapeDtypeStruct((SLOTS * 1024, 128), F32),
        in_specs=[pl.BlockSpec((PLACE_ROWS, 128), lambda j: (j, 0)), VM],
        out_specs=pl.BlockSpec((PLACE_ROWS, 128), lambda j: (j, 0)),
        name="place",
    )(moved, fin)


def on_device(
    pool_states, inner_window, state_window, move_plan, active_mask, inputs_inner, inputs_state, gate_rows,
    step_raw, lengths, conv_weight, conv_bias, step_bias, decay_log, skip_weight, norm_weight,
):
    my = lax.axis_index("seq")
    match = (move_plan[None, :, 0] == jnp.arange(32, dtype=I32)[:, None]).astype(I32)
    slot = jnp.sum(match * jnp.arange(SLOTS, dtype=I32)[None, :], axis=1)
    keep = jnp.sum(match * active_mask[None, :], axis=1)
    tag = jnp.sum(match * (move_plan[None, :, 1] + 1), axis=1)
    meta = jnp.stack([slot, keep], axis=1)
    tags = jnp.broadcast_to(tag[:, None, None], (32, 1, 128))
    tag_b = jnp.moveaxis(tag.reshape(4, 4, 2), 1, 0).reshape(4, 8)
    tags_b = jnp.broadcast_to(tag_b[:, :, None, None], (4, 8, 1, 128))
    blank = jnp.zeros((SLOTS, 3, 64), BF16)
    odd = (my % 2) == 1
    lane_window = jnp.concatenate(
        [jnp.where(odd, blank, state_window), jnp.where(odd, state_window, blank)], axis=2)
    win = jnp.concatenate(
        [inner_window.reshape(SLOTS, 24, 128), jnp.zeros((SLOTS, 5, 128), BF16), lane_window], axis=1)
    moved, wout, fin, mix = exchange(
        meta, lengths, skip_weight, tags, tags_b, pool_states.reshape(SLOTS, 1024, 128), win,
        inputs_inner[0], inputs_state[0], gate_rows[0], step_raw[0],
        conv_weight, conv_bias[None], step_bias[None], decay_log[None], norm_weight[None],
    )
    new_states = place(moved.reshape(SLOTS * 1024, 128), fin).reshape(SLOTS, 16, 64, 128)
    kept_st = jnp.concatenate([wout[1, 3:6], wout[2, 3:6]], axis=1)
    kept_st = lax.dynamic_slice_in_dim(kept_st, my * 64, 64, 1)[None]
    rows = jnp.concatenate([wout[0:1], wout[3:]], axis=0)
    new_in = rows[:, 0:24].reshape(SLOTS, 3, 1024).astype(BF16)
    moved_st = wout[3:, 29:32]
    moved_st = jnp.where(odd, moved_st[:, :, 64:], moved_st[:, :, :64])
    new_st = jnp.concatenate([kept_st, moved_st], axis=0).astype(BF16)
    return (new_states, new_in, new_st, mix[None])


def solution(mesh):
    return jax.shard_map(
        on_device,
        mesh=mesh,
        in_specs=(
            P("req", "seq", None, None), P("req", None, "seq"), P("req", None, "seq"), P("req", None), P("req"),
            P("req", "seq", None), P("req", "seq", None), P("req", "seq", None), P("req", "seq", None), P("req"),
            P(), P(), P(), P(), P(), P(),
        ),
        out_specs=(
            P("req", "seq", None, None), P("req", None, "seq"), P("req", None, "seq"), P("req", "seq", None),
        ),
        check_vma=False,
    )
```

time: 244 us -> 152 us (0.62); the launches traced: 241 us -> 152 us
  Pallas kernels: 204 us -> 132 us
  local copies, waits for them, and re-layouts: 29 us -> 13.2 us
    pallas_call x2 -> x1, Pallas kernels: 61.5 us -> 5.43 us  [place(): pl.pallas_call(place_kernel, grid=(4,), out_shape=jax.ShapeDtypeStruct((S...]
    pallas_call x1, Pallas kernels: 142 us -> 127 us  [exchange(): pl.pallas_call(exchange_kernel, out_shape=out_shape, in_specs=[SM, SM, SM...]
    unnamed x42 -> x5, local copies, waits for them, and re-layouts: 15.5 us -> 8.54 us
    slice x13 -> x2, local copies, waits for them, and re-layouts: 5.64 us -> 0.01 us  [on_device(): rows = jnp.concatenate([wout[0:1], wout[3:]], axis=0)]
where the time goes in v2:
time: 152 us
  Pallas kernels  132 us (87%)
  local copies, waits for them, and re-layouts  13.2 us (9%)
  other arithmetic  5 us (3%)
    pallas_call x1, Pallas kernels, exchange(): pl.pallas_call(exchange_kernel, out_shape=out_shape, in_specs=[SM, SM, SM...  127 us
    unnamed x5, local copies, waits for them, and re-layouts  8.54 us
    pallas_call x1, Pallas kernels, place(): pl.pallas_call(place_kernel, grid=(4,), out_shape=jax.ShapeDtypeStruct((S...  5.43 us

profile of v2, /device:TPU:1, one launch (start us, length us, event | category | flops | bytes accessed | tf_op | source)
XLA Modules:
  0.0 151.9 jit_solution(1372348497647746016)
XLA Ops:
  1.3 0.1 pad.7.clone
  1.4 0.8 slice_bitcast_fusion.2
  2.1 0.7 select_reduce_fusion
  2.9 0.1 reshape.42
  3.0 0.1 copy.49
  3.1 0.1 copy.50
  3.2 0.7 broadcast_in_dim.43.tags_b
  3.9 0.7 copy.55.meta
  4.6 0.7 broadcast_in_dim.41.tags
  5.3 1.3 broadcast_in_dim.46.conv_b
  6.6 0.7 broadcast_select_fusion.1
  7.3 1.0 copy.51
  8.3 0.1 reshape.44
  8.4 0.7 maximum_maximum_fusion.win
  9.1 1.6 %copy.54 = bf16[1,512,64]{2,1,0:T(8,128)(2,1)} copy(bf16[1,512,64]{1,2,0:T(8,128)(2,1)} %param.24) | data formatting | bytes 131072 | tf_op args[8]
  10.7 126.9 %exchange.1 = (bf16[13,1024,128]{2,1,0:T(8,128)(2,1)}, f32[15,32,128]{2,1,0:T(8,128)}, f32[1024,128]{1,0:T(8,128)}, bf16[512,4096]{1,0:T(8,128)(2,1)}) custom-call(s32[32,2]{1,0:T(8,128)} %copy.55.meta, s32[1]{0:T(128)S(6)} %copy.61.lens, f32[64]{0:T(128)} %skip.1, s32[32,1,128]{2,1,0:T(1,128)} %broadcast_in_dim.41.tags, ...), custom_call_target="tpu_custom_call" | custom-call | tf_op jit(solution)/shard_map/exchange/pallas_call | solution.py:611
  137.7 0.7 slice_bitcast_fusion.1
  138.4 0.1 fusion.2
  138.4 1.0 select_convert_fusion
  139.4 1.0 convert.14
  140.4 0.6 copy.57
  141.0 0.7 copy.56
  141.7 5.4 %place.1 = f32[13312,128]{1,0:T(8,128)} custom-call(bf16[13312,128]{1,0:T(8,128)(2,1)} %bitcast.30, f32[1024,128]{1,0:T(8,128)} %get-tuple-element.9.fin), custom_call_target="tpu_custom_call" | custom-call | tf_op jit(solution)/shard_map/place/pallas_call | solution.py:636
  147.2 4.7 %copy.62 = bf16[1,512,4096]{2,1,0:T(8,128)(2,1)} copy(bf16[1,512,4096]{2,1,0:T(8,128)(2,1)} %bitcast.27) | data formatting | bytes 8388608
  (7 shorter events, 0.1 us)

commit v3 on v2

--- a/solution.py
+++ b/solution.py
@@ -77,8 +77,9 @@
 
 
 def exchange_kernel(
-    meta, lens, skip, tags, tags_b, pool, win, xin, xst, gate, step, conv_w, conv_b, step_b, decay, norm_w,
-    moved, wout, fin_out, mix,
+    plan, mask, lens, skip, pool, iw, sw, xin, xst, gate, step, conv_w, conv_b, step_b, decay,
+    moved, wout, fin_out, mix, scale_out,
+    meta, tags, tags_b, win, tot_buf,
     stage, sbuf_a, sbuf_b, rel_a, rel_b, near_a, near_b, far_a, far_b, xbuf, xsbuf, gbuf, y_buf, read_buf, cum_buf, st_buf,
     lsend, lrecv, ssend, srecv, tbuf, tagbuf, rtag_a, rtag_b, tag_s, rtag_as, rtag_bs,
     cum3, cumt, dt2, sc_buf, wt_buf, base_buf, wtile, fin_buf, wstage, ffin, ffst, ffdt,
@@ -113,6 +114,36 @@
         pl.semaphore_signal(barrier, inc=1, device_id=(peer, my), device_id_type=MESH)
     for r in range(1, 4):
         pl.semaphore_signal(barrier, inc=1, device_id=(me, (my + r) % 4), device_id_type=MESH)
+
+    def table_body(d, carry):
+        slot, keep, tag = jnp.int32(0), jnp.int32(0), jnp.int32(0)
+        for k in range(SLOTS):
+            hit = plan[k, 0] == d
+            slot = jnp.where(hit, k, slot)
+            keep = jnp.where(hit, mask[k], keep)
+            tag = jnp.where(hit, plan[k, 1] + 1, tag)
+        meta[0, d] = slot
+        meta[1, d] = keep
+        row = jnp.full((1, 128), tag, I32)
+        tags[d] = row
+        tags_b[(d // 2) % 4, (d // 8) * 2 + d % 2] = row
+        return carry
+
+    lax.fori_loop(0, 32, table_body, 0)
+
+    def window_body(k, carry):
+        rows3 = iw[k].astype(F32)
+        for i in range(3):
+            for q in range(8):
+                win[k, pl.ds(i * 8 + q, 1), :] = rows3[i : i + 1, q * 128 : (q + 1) * 128]
+        win[k, pl.ds(24, 8), :] = jnp.zeros((8, 128), F32)
+        own = sw[k].astype(F32)
+        blank = jnp.zeros((3, 64), F32)
+        win[k, pl.ds(29, 3), :] = jnp.where(
+            my % 2 == 1, jnp.concatenate([blank, own], axis=1), jnp.concatenate([own, blank], axis=1))
+        return carry
+
+    lax.fori_loop(0, SLOTS, window_body, 0)
     pl.semaphore_wait(barrier, 34)
 
     def send(src, dst, ssem, rsem, dev):
@@ -137,10 +168,10 @@
         cp.wait()
 
     def fill(ref, lead, q, dest, half):
-        slot = meta[dest, 0]
-        keep = meta[dest, 1].astype(F32)
+        slot = meta[0, dest]
+        keep = meta[1, dest].astype(F32)
         ref[lead, q, pl.ds(0, 512), :] = (stage[slot, pl.ds(512 * half, 512), :] * keep).astype(BF16)
-        ref[lead, q, pl.ds(512, 16), :] = (win[slot, pl.ds(16 * half, 16), :].astype(F32) * keep).astype(BF16)
+        ref[lead, q, pl.ds(512, 16), :] = (win[slot, pl.ds(16 * half, 16), :] * keep).astype(BF16)
 
     def fill_a(ref, lead, xd):
         def one(q, carry):
@@ -305,6 +336,34 @@
         lends.append(send(lsend.at[(my + r) % 4], lrecv.at[my], lend_send.at[r], lend_recv.at[r], dev))
         lends.append(send(tbuf.at[my], tbuf.at[my], lend_send.at[4 + r], lend_recv.at[4 + r], dev))
 
+    @pl.when(my == 0)
+    def _():
+        rowc = lax.broadcasted_iota(I32, (16, HEADS), 0)
+        cum_buf[pl.ds(0, 16), :] = jnp.where(rowc < 3, -1.0e6, cum_buf[pl.ds(0, 16), :])
+
+    gate_load.wait()
+
+    def ready_body(k, carry):
+        r0 = pl.multiple_of(k * CHUNK, CHUNK)
+        cum3[...] = jnp.concatenate(split3(cum_buf[pl.ds(r0, CHUNK), :]), axis=1)
+        rowpos = my * SPAN + r0 + lax.broadcasted_iota(I32, (CHUNK, 128), 0)
+
+        def group_body(j, inner):
+            lanes = [pl.ds(pl.multiple_of(j * 256 + g * 128, 128), 128) for g in range(2)]
+            valid = (rowpos < length).astype(F32)
+            ce = [nn(cum3[...], pick_lanes(3, 2 * j + g)) for g in range(2)]
+            gates = [silu(gbuf[pl.ds(r0, CHUNK), lanes[g]].astype(F32)) * valid for g in range(2)]
+            for g in range(2):
+                xbuf[pl.ds(r0, CHUNK), lanes[g]] = jnp.exp2(ce[g]).astype(BF16)
+                gbuf[pl.ds(r0, CHUNK), lanes[g]] = gates[g].astype(BF16)
+            return inner
+
+        lax.fori_loop(0, PAIRS // 2, group_body, 0)
+        return carry
+
+    lax.fori_loop(0, CHUNKS, ready_body, 0)
+    tot_buf[...] = jnp.zeros_like(tot_buf)
+
     for cp in rtags:
         cp.wait()
     tag_loads = [
@@ -329,8 +388,8 @@
             ta, tb = targets(e)
             first_a, first_b = jnp.int32(0), jnp.int32(0)
             for q in (1, 2, 3):
-                first_a = first_a + jnp.where(rtag_as[(mx + 4 - q) % 4, ta, 0, 0] == 1, q, 0)
-                first_b = first_b + jnp.where(rtag_bs[(mz + 4 - q) % 4, tb, 0, 0] == 1, q, 0)
+                first_a = jnp.where(rtag_as[(mx + 4 - q) % 4, ta, 0, 0] == 1, q, first_a)
+                first_b = jnp.where(rtag_bs[(mz + 4 - q) % 4, tb, 0, 0] == 1, q, first_b)
             block_a = rel_a[(mx + 4 - swapped(first_a, p)) % 4, ta]
             block_b = rel_b[(mz + 4 - swapped(first_b, p)) % 4, tb]
             if e == 0:
@@ -350,7 +409,7 @@
     def source_of(j):
         acc = jnp.int32(0)
         for s in range(32):
-            acc = acc + jnp.where(tag_s[s, 0, 0] == j + 1, s, 0)
+            acc = jnp.where(tag_s[s, 0, 0] == j + 1, s, acc)
         return acc
 
     def split_source(src):
@@ -475,63 +534,44 @@
         outs.append(cp)
 
     put_out(fin_buf, fin_out, 30)
-    gate_load.wait()
-    for cp in sins:
-        cp.wait()
-
-    @pl.when(my == 0)
-    def _():
-        rowc = lax.broadcasted_iota(I32, (16, HEADS), 0)
-        cum_buf[pl.ds(0, 16), :] = jnp.where(rowc < 3, -1.0e6, cum_buf[pl.ds(0, 16), :])
-
-        def patch(i, carry):
-            lanes = pl.ds(pl.multiple_of(i * 256, 256), 256)
-            new = srecv[i // 4, pl.ds(128, 16), pl.ds(pl.multiple_of((i % 4) * 256, 256), 256)].astype(F32)
-            old = y_buf[pl.ds(0, 16), lanes].astype(F32)
-            rowy = lax.broadcasted_iota(I32, (16, 256), 0)
-            y_buf[pl.ds(0, 16), lanes] = jnp.where(rowy < 3, new, old).astype(BF16)
+    def quarter(owner):
+        base = owner * 1024
+
+        @pl.when(my == 0)
+        def _():
+            for j in range(4):
+                lanes = pl.ds(pl.multiple_of(base + j * 256, 128), 256)
+                new = srecv[owner, pl.ds(128, 16), pl.ds(j * 256, 256)].astype(F32)
+                old = y_buf[pl.ds(0, 16), lanes].astype(F32)
+                rowy = lax.broadcasted_iota(I32, (16, 256), 0)
+                y_buf[pl.ds(0, 16), lanes] = jnp.where(rowy < 3, new, old).astype(BF16)
+
+        def group_body(j, carry):
+            lanes = pl.ds(pl.multiple_of(base + j * 256, 128), 256)
+            state = srecv[owner, pl.ds(0, 128), pl.ds(pl.multiple_of(j * 256, 256), 256)]
+            spans = [pl.ds(r * CHUNK, CHUNK) for r in range(CHUNKS)]
+            parts = [nn(read_buf[span, :], state) for span in spans]
+            new, squares = [], []
+            for span, part in zip(spans, parts):
+                y = y_buf[span, lanes].astype(F32) + xbuf[span, lanes].astype(F32) * part
+                v = y.astype(BF16).astype(F32) * gbuf[span, lanes].astype(F32)
+                new.append(v.astype(BF16))
+                squares.append(tot_buf[span, :] + v[:, 0:128] * v[:, 0:128] + v[:, 128:256] * v[:, 128:256])
+            for span, v, square in zip(spans, new, squares):
+                y_buf[span, lanes] = v
+                tot_buf[span, :] = square
             return carry
 
-        lax.fori_loop(0, INNER // 256, patch, 0)
-
-    def tail_body(k, carry):
-        r0 = pl.multiple_of(k * CHUNK, CHUNK)
-        cum3[...] = jnp.concatenate(split3(cum_buf[pl.ds(r0, CHUNK), :]), axis=1)
-        rowpos = my * SPAN + r0 + lax.broadcasted_iota(I32, (CHUNK, 128), 0)
-
-        def group_body(j, total):
-            lanes = [pl.ds(pl.multiple_of(j * 256 + g * 128, 128), 128) for g in range(2)]
-            owner = j // 4
-            valid = (rowpos < length).astype(F32)
-            read = read_buf[pl.ds(r0, CHUNK), :]
-            own = [pl.ds(pl.multiple_of((j % 4) * 256 + g * 128, 128), 128) for g in range(2)]
-            ce = [nn(cum3[...], pick_lanes(3, 2 * j + g)) for g in range(2)]
-            part = [nn(read, srecv[owner, pl.ds(0, 128), own[g]]) for g in range(2)]
-            old = [y_buf[pl.ds(r0, CHUNK), lanes[g]].astype(F32) for g in range(2)]
-            gates = [silu(gbuf[pl.ds(r0, CHUNK), lanes[g]].astype(F32)) for g in range(2)]
-            new = []
-            for g in range(2):
-                y = (old[g] + jnp.exp2(ce[g]) * part[g]) * valid
-                new.append(y.astype(BF16).astype(F32) * gates[g])
-            for g in range(2):
-                st_buf[:, lanes[g]] = new[g]
-                total = total + new[g] * new[g]
-            return total
-
-        total = lax.fori_loop(0, PAIRS // 2, group_body, jnp.zeros((CHUNK, 128), F32))
-        sc_buf[...] = jnp.broadcast_to(
-            lax.rsqrt(jnp.sum(total, axis=1, keepdims=True) * (1.0 / INNER) + EPSILON), (CHUNK, CHUNK))
-
-        def norm_body(i, inner):
-            lanes = pl.ds(pl.multiple_of(i * 128, 128), 128)
-            y_buf[pl.ds(r0, CHUNK), lanes] = (st_buf[:, lanes] * sc_buf[...] * norm_w[0:1, lanes]).astype(BF16)
-            return inner
-
-        lax.fori_loop(0, PAIRS, norm_body, 0)
-        return carry
-
-    lax.fori_loop(0, CHUNKS, tail_body, 0)
+        lax.fori_loop(0, 4, group_body, 0)
+
+    quarter(my)
+    for r in (1, 3, 2):
+        sins[r - 1].wait()
+        quarter((my + 4 - r) % 4)
     put_out(y_buf, mix, 31)
+    tot_buf[...] = jnp.broadcast_to(
+        lax.rsqrt(jnp.sum(tot_buf[...], axis=1, keepdims=True) * (1.0 / INNER) + EPSILON), (SPAN, 128))
+    put_out(tot_buf, scale_out, 29)
 
     spots = [places(j) for j in range(SLOTS)]
     for p in (2, 3):
@@ -551,7 +591,7 @@
         cp.wait()
 
 
-def exchange(meta, lens, skip, tags, tags_b, pool, win, xin, xst, gate, step, conv_w, conv_b, step_b, decay, norm_w):
+def exchange(*operands):
     dma = pltpu.SemaphoreType.DMA
     shape = jax.ShapeDtypeStruct
     out_shape = (
@@ -559,8 +599,14 @@
         shape((SLOTS + 2, 32, 128), F32),
         shape((1024, 128), F32),
         shape((SPAN, INNER), BF16),
+        shape((SPAN, 128), F32),
     )
     scratch = [
+        pltpu.SMEM((2, 32), I32),
+        pltpu.VMEM((32, 1, 128), I32),
+        pltpu.VMEM((4, 8, 1, 128), I32),
+        pltpu.VMEM((SLOTS, 32, 128), F32),
+        pltpu.VMEM((SPAN, 128), F32),
         pltpu.VMEM((SLOTS, 1024, 128), F32),
         pltpu.VMEM((4, 8, HALF, 128), BF16),
         pltpu.VMEM((4, 8, HALF, 128), BF16),
@@ -611,36 +657,47 @@
     return pl.pallas_call(
         exchange_kernel,
         out_shape=out_shape,
-        in_specs=[SM, SM, SM, VM, VM, ANY, VM, ANY, ANY, ANY, VM, VM, VM, VM, VM, VM],
+        in_specs=[SM, SM, SM, SM, ANY, VM, VM, ANY, ANY, ANY, VM, VM, VM, VM, VM],
         out_specs=[ANY] * len(out_shape),
         scratch_shapes=scratch,
         compiler_params=pltpu.CompilerParams(
             collective_id=1, has_side_effects=True, vmem_limit_bytes=67043328
         ),
         name="exchange",
-    )(meta, lens, skip, tags, tags_b, pool, win, xin, xst, gate, step, conv_w, conv_b, step_b, decay, norm_w)
+    )(*operands)
 
 
 PLACE_ROWS = SLOTS * 256
 
 
-def place_kernel(moved, fin, states):
+def place_kernel(moved, fin, gated, scale, norm_w, states, mixed):
     states[...] = moved[...].astype(F32)
 
     @pl.when(pl.program_id(0) == 0)
     def _():
         states[pl.ds(0, 1024), :] = fin[...]
 
-
-def place(moved, fin):
+    def norm_body(i, carry):
+        lanes = pl.ds(pl.multiple_of(i * 128, 128), 128)
+        mixed[:, lanes] = (gated[:, lanes].astype(F32) * scale[...] * norm_w[0:1, lanes]).astype(BF16)
+        return carry
+
+    lax.fori_loop(0, PAIRS, norm_body, 0)
+
+
+def place(moved, fin, gated, scale, norm_w):
+    rows = lambda count, lanes: pl.BlockSpec((count, lanes), lambda j: (j, 0))
     return pl.pallas_call(
         place_kernel,
         grid=(4,),
-        out_shape=jax.ShapeDtypeStruct((SLOTS * 1024, 128), F32),
-        in_specs=[pl.BlockSpec((PLACE_ROWS, 128), lambda j: (j, 0)), VM],
-        out_specs=pl.BlockSpec((PLACE_ROWS, 128), lambda j: (j, 0)),
+        out_shape=(
+            jax.ShapeDtypeStruct((SLOTS * 1024, 128), F32),
+            jax.ShapeDtypeStruct((SPAN, INNER), BF16),
+        ),
+        in_specs=[rows(PLACE_ROWS, 128), VM, rows(CHUNK, INNER), rows(CHUNK, 128), VM],
+        out_specs=[rows(PLACE_ROWS, 128), rows(CHUNK, INNER)],
         name="place",
-    )(moved, fin)
+    )(moved, fin, gated, scale, norm_w)
 
 
 def on_device(
@@ -648,26 +705,14 @@
     step_raw, lengths, conv_weight, conv_bias, step_bias, decay_log, skip_weight, norm_weight,
 ):
     my = lax.axis_index("seq")
-    match = (move_plan[None, :, 0] == jnp.arange(32, dtype=I32)[:, None]).astype(I32)
-    slot = jnp.sum(match * jnp.arange(SLOTS, dtype=I32)[None, :], axis=1)
-    keep = jnp.sum(match * active_mask[None, :], axis=1)
-    tag = jnp.sum(match * (move_plan[None, :, 1] + 1), axis=1)
-    meta = jnp.stack([slot, keep], axis=1)
-    tags = jnp.broadcast_to(tag[:, None, None], (32, 1, 128))
-    tag_b = jnp.moveaxis(tag.reshape(4, 4, 2), 1, 0).reshape(4, 8)
-    tags_b = jnp.broadcast_to(tag_b[:, :, None, None], (4, 8, 1, 128))
-    blank = jnp.zeros((SLOTS, 3, 64), BF16)
     odd = (my % 2) == 1
-    lane_window = jnp.concatenate(
-        [jnp.where(odd, blank, state_window), jnp.where(odd, state_window, blank)], axis=2)
-    win = jnp.concatenate(
-        [inner_window.reshape(SLOTS, 24, 128), jnp.zeros((SLOTS, 5, 128), BF16), lane_window], axis=1)
-    moved, wout, fin, mix = exchange(
-        meta, lengths, skip_weight, tags, tags_b, pool_states.reshape(SLOTS, 1024, 128), win,
+    moved, wout, fin, gated, scale = exchange(
+        move_plan, active_mask, lengths, skip_weight, pool_states.reshape(SLOTS, 1024, 128), inner_window, state_window,
         inputs_inner[0], inputs_state[0], gate_rows[0], step_raw[0],
-        conv_weight, conv_bias[None], step_bias[None], decay_log[None], norm_weight[None],
+        conv_weight, conv_bias[None], step_bias[None], decay_log[None],
     )
-    new_states = place(moved.reshape(SLOTS * 1024, 128), fin).reshape(SLOTS, 16, 64, 128)
+    new_states, mix = place(moved.reshape(SLOTS * 1024, 128), fin, gated, scale, norm_weight[None])
+    new_states = new_states.reshape(SLOTS, 16, 64, 128)
     kept_st = jnp.concatenate([wout[1, 3:6], wout[2, 3:6]], axis=1)
     kept_st = lax.dynamic_slice_in_dim(kept_st, my * 64, 64, 1)[None]
     rows = jnp.concatenate([wout[0:1], wout[3:]], axis=0)

time: 152 us -> 133 us (0.88)
  Pallas kernels: 132 us -> 120 us
  local copies, waits for them, and re-layouts: 13.2 us -> 9.23 us
  other arithmetic: 5 us -> 2.02 us
    pallas_call x1, Pallas kernels: 127 us -> 111 us  [exchange(): pl.pallas_call(exchange_kernel, out_shape=out_shape, in_specs=[SM, SM, SM...]
    pallas_call x1, Pallas kernels: 5.43 us -> 8.95 us  [place(): pl.pallas_call(place_kernel, grid=(4,), out_shape=(jax.ShapeDtypeStruct((...]
    unnamed x5 -> x6, local copies, waits for them, and re-layouts: 8.54 us -> 7.16 us
where the time goes in v3:
time: 133 us; the launch traced here: 132 us
  Pallas kernels  120 us (90%)
  local copies, waits for them, and re-layouts  9.23 us (7%)
  other arithmetic  2.02 us (2%)
  between operations  1.33 us (1%)
    pallas_call x1, Pallas kernels, exchange(): pl.pallas_call(exchange_kernel, out_shape=out_shape, in_specs=[SM, SM, SM...  111 us
    pallas_call x1, Pallas kernels, place(): pl.pallas_call(place_kernel, grid=(4,), out_shape=(jax.ShapeDtypeStruct((...  8.95 us
    unnamed x6, local copies, waits for them, and re-layouts  7.16 us

profile of v3, /device:TPU:1, one launch (start us, length us, event | category | flops | bytes accessed | tf_op | source)
XLA Modules:
  0.0 132.5 jit_solution(5618994684682057549)
XLA Ops:
  1.3 1.4 %copy.27.plan = s32[13,2]{1,0:T(8,128)} copy(s32[13,2]{0,1:T(2,128)} %param.19) | data formatting | bytes 208 | tf_op args[3]
  2.6 1.3 copy.29.sw
  4.0 1.3 %broadcast_in_dim.19.conv_b = f32[1,4352]{1,0:T(1,128)} reshape(f32[4352]{0:T(1024)} %param.27) | data formatting | bytes 34816 | tf_op jit(solution)/shard_map/broadcast_in_dim | solution.py:712
  5.3 1.6 %copy.28.iw = bf16[13,3,1024]{2,1,0:T(4,128)(2,1)} copy(bf16[13,3,1024]{2,0,1:T(8,128)(2,1)} %param.17) | data formatting | bytes 159744 | tf_op args[1]
  6.9 1.6 %copy.26 = bf16[1,512,64]{2,1,0:T(8,128)(2,1)} copy(bf16[1,512,64]{1,2,0:T(8,128)(2,1)} %param.24) | data formatting | bytes 131072 | tf_op args[8]
  8.5 110.9 %exchange.1 = (bf16[13,1024,128]{2,1,0:T(8,128)(2,1)}, f32[15,32,128]{2,1,0:T(8,128)}, f32[1024,128]{1,0:T(8,128)}, bf16[512,4096]{1,0:T(8,128)(2,1)}, f32[512,128]{1,0:T(8,128)}) custom-call(s32[13,2]{1,0:T(8,128)} %copy.27.plan, s32[13]{0:T(128)} %mask.1, s32[1]{0:T(128)S(6)} %copy.32.lens, f32[64]{0:T(128)} %skip.1, f32[13,1024,128]{2,1,0:T(8,128)} %bitcast.17, ...), custom_call_target="tpu_custom_call" | custom-call | tf_op jit(solution)/shard_map/exchange/pallas_call | solution.py:657
  119.5 0.7 slice_bitcast_fusion.1
  120.1 0.1 fusion.2
  120.2 1.0 select_convert_fusion
  121.2 1.0 convert.14
  122.2 0.6 copy.31
  122.8 0.7 copy.30
  123.5 9.0 %place.1 = (f32[13312,128]{1,0:T(8,128)}, bf16[512,4096]{1,0:T(8,128)(2,1)}) custom-call(bf16[13312,128]{1,0:T(8,128)(2,1)} %bitcast.20, f32[1024,128]{1,0:T(8,128)} %get-tuple-element.12.fin, bf16[512,4096]{1,0:T(8,128)(2,1)} %get-tuple-element.13.gated, f32[512,128]{1,0:T(8,128)} %get-tuple-element.14.scale, f32[1,4096]{1,0:T(1,128)} %bitcast.23), custom_call_target="tpu_custom_call" | custom-call | tf_op jit(solution)/shard_map/place/pallas_call | solution.py:690
  (5 shorter events, 0.1 us)

commit v4 on v3

--- a/solution.py
+++ b/solution.py
@@ -118,10 +118,10 @@
     def table_body(d, carry):
         slot, keep, tag = jnp.int32(0), jnp.int32(0), jnp.int32(0)
         for k in range(SLOTS):
-            hit = plan[k, 0] == d
+            hit = plan[0, k] == d
             slot = jnp.where(hit, k, slot)
             keep = jnp.where(hit, mask[k], keep)
-            tag = jnp.where(hit, plan[k, 1] + 1, tag)
+            tag = jnp.where(hit, plan[1, k] + 1, tag)
         meta[0, d] = slot
         meta[1, d] = keep
         row = jnp.full((1, 128), tag, I32)
@@ -131,19 +131,18 @@
 
     lax.fori_loop(0, 32, table_body, 0)
 
-    def window_body(k, carry):
-        rows3 = iw[k].astype(F32)
-        for i in range(3):
+    for k in range(SLOTS):
+        win[k, pl.ds(24, 8), :] = jnp.zeros((8, 128), F32)
+    for i in range(3):
+        block = iw[i].astype(F32)
+        own = sw[i].astype(F32)
+        blank = jnp.zeros((SLOTS, 64), F32)
+        wide = jnp.where(
+            my % 2 == 1, jnp.concatenate([blank, own], axis=1), jnp.concatenate([own, blank], axis=1))
+        for k in range(SLOTS):
             for q in range(8):
-                win[k, pl.ds(i * 8 + q, 1), :] = rows3[i : i + 1, q * 128 : (q + 1) * 128]
-        win[k, pl.ds(24, 8), :] = jnp.zeros((8, 128), F32)
-        own = sw[k].astype(F32)
-        blank = jnp.zeros((3, 64), F32)
-        win[k, pl.ds(29, 3), :] = jnp.where(
-            my % 2 == 1, jnp.concatenate([blank, own], axis=1), jnp.concatenate([own, blank], axis=1))
-        return carry
-
-    lax.fori_loop(0, SLOTS, window_body, 0)
+                win[k, pl.ds(i * 8 + q, 1), :] = block[k : k + 1, q * 128 : (q + 1) * 128]
+            win[k, pl.ds(29 + i, 1), :] = wide[k : k + 1]
     pl.semaphore_wait(barrier, 34)
 
     def send(src, dst, ssem, rsem, dev):
@@ -162,7 +161,7 @@
         dev = (me, (my + r) % 4)
         firsts.append(send(xin.at[pl.ds(0, 16)], ffin.at[my], f_send.at[r], f_recv.at[r], dev))
         firsts.append(send(xst.at[pl.ds(0, 16)], ffst.at[my], f_send.at[4 + r], f_recv.at[4 + r], dev))
-        firsts.append(send(step.at[pl.ds(0, 16)], ffdt.at[my], f_send.at[8 + r], f_recv.at[8 + r], dev))
+        firsts.append(send(step.at[:, pl.ds(0, 128)], ffdt.at[my], f_send.at[8 + r], f_recv.at[8 + r], dev))
 
     for cp in loads:
         cp.wait()
@@ -188,7 +187,7 @@
         lax.fori_loop(0, 8, one, 0)
 
     phase_a, phase_b, rtags = {}, {}, []
-    for d in (2, 1, 3):
+    for d in (1, 3, 2):
         xd, zd = (mx + d) % 4, (mz + d) % 4
         dev_a, dev_b = (at(d, 0, 0), my), (at(0, d, 0), my)
         fill_a(sbuf_a, xd, xd)
@@ -221,7 +220,7 @@
         ct = (mc + dc) % 2
         return ((mz + de) % 4) * 2 + ct, ((mx + de) % 4) * 2 + ct
 
-    for e in range(1, 8):
+    for e in (2, 6, 3, 7, 1, 4, 5):
         ta, tb = targets(e)
         forward(0, e, rel_a.at[mx, ta], rel_b.at[mz, tb])
     row_a(0)[...] = rel_a[mx, mz * 2 + mc]
@@ -253,7 +252,7 @@
         r0 = pl.multiple_of(k * CHUNK, CHUNK)
         pos = my * SPAN + r0 + lax.broadcasted_iota(I32, (CHUNK, HEADS), 0)
         live = ((pos < length) & (pos >= 3)).astype(F32)
-        dt = softplus(step[pl.ds(r0, CHUNK), :].astype(F32) + step_b[0:1, :]) * live
+        dt = softplus(jnp.transpose(step[:, pl.ds(r0, CHUNK)].astype(F32)) + step_b[0:1, :]) * live
         rate = dt * (-LOG2E * jnp.exp(decay[0:1, :]))
         rows = lax.broadcasted_iota(I32, (CHUNK, CHUNK), 0)
         cols = lax.broadcasted_iota(I32, (CHUNK, CHUNK), 1)
@@ -267,7 +266,7 @@
         cum_buf[pl.ds(r0, CHUNK), :] = cum + base_buf[0:1, 0:HEADS]
         base_buf[0:1, 0:HEADS] = base_buf[0:1, 0:HEADS] + cum[CHUNK - 1 : CHUNK, :]
         xs_tile = xsbuf[pl.ds(r0, CHUNK + 16), :].astype(F32)
-        mixed = conv_tile(xs_tile, conv_w[:, INNER : INNER + 256], conv_b[0:1, INNER : INNER + 256], CHUNK)
+        mixed = conv_tile(xs_tile, conv_w[:, INNER : INNER + 256], jnp.concatenate([conv_b[32:33, :], conv_b[33:34, :]], axis=1), CHUNK)
         write, read = mixed[:, 0:128], mixed[:, 128:256]
         read_buf[pl.ds(r0, CHUNK), :] = read
         sc_buf[...] = jnp.where(rows >= cols, nt(read, write), 0.0)
@@ -284,7 +283,7 @@
             both = [nn(cum3[...], pick_heads(3, pairs[g])) for g in every]
             dte = [nn(dt2[...], pick_lanes(2, pairs[g])) for g in every]
             carried = [nn(read_buf[pl.ds(r0, CHUNK), :], state[g].astype(BF16)) for g in every]
-            value = [conv_tile(x[g], conv_w[:, lanes[g]], conv_b[0:1, lanes[g]], CHUNK).astype(F32) for g in every]
+            value = [conv_tile(x[g], conv_w[:, lanes[g]], conv_b[pl.ds(pairs[g], 1), :], CHUNK).astype(F32) for g in every]
             ys, states = [], []
             for g in every:
                 sc = sc_buf[...]
@@ -384,7 +383,7 @@
         return jnp.where(first == p, 1, p)
 
     for p in (1, 2, 3):
-        for e in range(8):
+        for e in (2, 6, 3, 7, 0, 1, 4, 5):
             ta, tb = targets(e)
             first_a, first_b = jnp.int32(0), jnp.int32(0)
             for q in (1, 2, 3):
@@ -440,7 +439,7 @@
     ]
     for cp in own_first:
         cp.start()
-    ffdt[my] = step[pl.ds(0, 16), :]
+    ffdt[my] = step[:, 0:128]
     for cp in own_first:
         cp.wait()
     for cp in lends:
@@ -458,7 +457,7 @@
 
     posf = lax.broadcasted_iota(I32, (16, HEADS), 0)
     livef = ((posf < length) & (posf < 3)).astype(F32)
-    dtf0 = softplus(ffdt[0].astype(F32) + step_b[0:1, :]) * livef
+    dtf0 = softplus(jnp.transpose(ffdt[0].astype(F32))[0:16] + step_b[0:1, :]) * livef
     rate0 = dtf0 * (-LOG2E * jnp.exp(decay[0:1, :]))
     c0 = rate0[0:1]
     c1 = c0 + rate0[1:2]
@@ -475,7 +474,7 @@
     w_low = wtile[0].astype(F32) + wtile[1].astype(F32)
     w_high = wtile[2].astype(F32) + wtile[3].astype(F32)
     e_st = jnp.concatenate([jnp.concatenate([w_low, w_high], axis=1), ffst[0].astype(F32)], axis=0)
-    mixed0 = conv_tile(e_st, conv_w[:, INNER : INNER + 256], conv_b[0:1, INNER : INNER + 256], 16)
+    mixed0 = conv_tile(e_st, conv_w[:, INNER : INNER + 256], jnp.concatenate([conv_b[32:33, :], conv_b[33:34, :]], axis=1), 16)
     write0, read0 = mixed0[:, 0:128], mixed0[:, 128:256]
     read0_buf[...] = read0
     sc0_buf[...] = nt(read0, write0)
@@ -499,7 +498,7 @@
         x0 = jnp.concatenate([wq, ffin[0, :, lanes].astype(F32)], axis=0)
         small = nn(small3[...], pick_lanes(3, i))
         cf, dtf, totl = small[0:16], small[16:32], small[32:48]
-        v0 = conv_tile(x0, conv_w[:, lanes], conv_b[0:1, lanes], 16).astype(F32)
+        v0 = conv_tile(x0, conv_w[:, lanes], conv_b[pl.ds(i, 1), :], 16).astype(F32)
         vd = v0 * dtf
         scaled = jnp.concatenate([jnp.exp2(cf[2:3] - cf) * vd, jnp.zeros((112, 128), F32)], axis=0).astype(BF16)
         carry = jnp.exp2(cf[2:3]) * s0t + nn(w0t[...], scaled)
@@ -645,7 +644,7 @@
         pltpu.VMEM((SLOTS + 2, 32, 128), F32),
         pltpu.VMEM((4, 16, INNER), BF16),
         pltpu.VMEM((4, 16, 256), BF16),
-        pltpu.VMEM((4, 16, HEADS), BF16),
+        pltpu.VMEM((4, HEADS, 128), BF16),
         pltpu.VMEM((48, 192), BF16),
         pltpu.VMEM((128, 128), BF16),
         pltpu.VMEM((16, 128), BF16),
@@ -667,60 +666,75 @@
     )(*operands)
 
 
-PLACE_ROWS = SLOTS * 256
-
-
-def place_kernel(moved, fin, gated, scale, norm_w, states, mixed):
+STEPS = 8
+PLACE_ROWS = SLOTS * 1024 // STEPS
+MIX_ROWS = SPAN // STEPS
+
+
+def place_kernel(moved, fin, gated, scale, norm_w, wout, states, mixed, win_in, win_st, acc_in, acc_st):
+    my = lax.axis_index("seq")
     states[...] = moved[...].astype(F32)
 
     @pl.when(pl.program_id(0) == 0)
     def _():
         states[pl.ds(0, 1024), :] = fin[...]
+        for j in range(SLOTS):
+            src = 0 if j == 0 else 2 + j
+            for i in range(3):
+                for q in range(8):
+                    acc_in[i, pl.ds(j, 1), pl.ds(q * 128, 128)] = wout[src, pl.ds(i * 8 + q, 1), :]
+                if j == 0:
+                    acc_st[i, pl.ds(0, 1), :] = jnp.where(my >= 2, wout[2, pl.ds(3 + i, 1), :], wout[1, pl.ds(3 + i, 1), :])
+                else:
+                    acc_st[i, pl.ds(j, 1), :] = wout[src, pl.ds(29 + i, 1), :]
+        for i in range(3):
+            win_in[i] = acc_in[i].astype(BF16)
+            rows = acc_st[i]
+            win_st[i] = jnp.where(my % 2 == 1, rows[:, 64:128], rows[:, 0:64]).astype(BF16)
 
     def norm_body(i, carry):
         lanes = pl.ds(pl.multiple_of(i * 128, 128), 128)
-        mixed[:, lanes] = (gated[:, lanes].astype(F32) * scale[...] * norm_w[0:1, lanes]).astype(BF16)
+        mixed[:, lanes] = (gated[:, lanes].astype(F32) * scale[...] * norm_w[pl.ds(i, 1), :]).astype(BF16)
         return carry
 
-    lax.fori_loop(0, PAIRS, norm_body, 0)
-
-
-def place(moved, fin, gated, scale, norm_w):
+    lax.fori_loop(0, PAIRS, norm_body, 0, unroll=4)
+
+
+def place(moved, fin, gated, scale, norm_w, wout):
     rows = lambda count, lanes: pl.BlockSpec((count, lanes), lambda j: (j, 0))
+    whole = lambda lanes: pl.BlockSpec((3, SLOTS, lanes), lambda j: (0, 0, 0))
     return pl.pallas_call(
         place_kernel,
-        grid=(4,),
+        grid=(STEPS,),
         out_shape=(
             jax.ShapeDtypeStruct((SLOTS * 1024, 128), F32),
             jax.ShapeDtypeStruct((SPAN, INNER), BF16),
+            jax.ShapeDtypeStruct((3, SLOTS, 1024), BF16),
+            jax.ShapeDtypeStruct((3, SLOTS, 64), BF16),
         ),
-        in_specs=[rows(PLACE_ROWS, 128), VM, rows(CHUNK, INNER), rows(CHUNK, 128), VM],
-        out_specs=[rows(PLACE_ROWS, 128), rows(CHUNK, INNER)],
+        in_specs=[rows(PLACE_ROWS, 128), VM, rows(MIX_ROWS, INNER), rows(MIX_ROWS, 128), VM, VM],
+        out_specs=[rows(PLACE_ROWS, 128), rows(MIX_ROWS, INNER), whole(1024), whole(64)],
+        scratch_shapes=[pltpu.VMEM((3, SLOTS, 1024), F32), pltpu.VMEM((3, SLOTS, 128), F32)],
         name="place",
-    )(moved, fin, gated, scale, norm_w)
+    )(moved, fin, gated, scale, norm_w, wout)
 
 
 def on_device(
     pool_states, inner_window, state_window, move_plan, active_mask, inputs_inner, inputs_state, gate_rows,
     step_raw, lengths, conv_weight, conv_bias, step_bias, decay_log, skip_weight, norm_weight,
 ):
-    my = lax.axis_index("seq")
-    odd = (my % 2) == 1
     moved, wout, fin, gated, scale = exchange(
-        move_plan, active_mask, lengths, skip_weight, pool_states.reshape(SLOTS, 1024, 128), inner_window, state_window,
-        inputs_inner[0], inputs_state[0], gate_rows[0], step_raw[0],
-        conv_weight, conv_bias[None], step_bias[None], decay_log[None],
+        move_plan.T, active_mask, lengths, skip_weight, pool_states.reshape(SLOTS, 1024, 128),
+        jnp.transpose(inner_window, (1, 0, 2)), jnp.transpose(state_window, (1, 0, 2)),
+        inputs_inner[0], inputs_state[0], gate_rows[0], step_raw[0].T,
+        conv_weight, conv_bias.reshape(34, 128), step_bias[None], decay_log[None],
     )
-    new_states, mix = place(moved.reshape(SLOTS * 1024, 128), fin, gated, scale, norm_weight[None])
-    new_states = new_states.reshape(SLOTS, 16, 64, 128)
-    kept_st = jnp.concatenate([wout[1, 3:6], wout[2, 3:6]], axis=1)
-    kept_st = lax.dynamic_slice_in_dim(kept_st, my * 64, 64, 1)[None]
-    rows = jnp.concatenate([wout[0:1], wout[3:]], axis=0)
-    new_in = rows[:, 0:24].reshape(SLOTS, 3, 1024).astype(BF16)
-    moved_st = wout[3:, 29:32]
-    moved_st = jnp.where(odd, moved_st[:, :, 64:], moved_st[:, :, :64])
-    new_st = jnp.concatenate([kept_st, moved_st], axis=0).astype(BF16)
-    return (new_states, new_in, new_st, mix[None])
+    new_states, mix, new_in, new_st = place(
+        moved.reshape(SLOTS * 1024, 128), fin, gated, scale, norm_weight.reshape(32, 128), wout)
+    return (
+        new_states.reshape(SLOTS, 16, 64, 128), jnp.transpose(new_in, (1, 0, 2)), jnp.transpose(new_st, (1, 0, 2)),
+        mix[None],
+    )
 
 
 def solution(mesh):

time: 133 us -> 124 us (0.932)
  local copies, waits for them, and re-layouts: 9.23 us -> 0 us
  other arithmetic: 2.02 us -> 0 us
  Pallas kernels: 120 us -> 122 us
    unnamed x6 -> x0, local copies, waits for them, and re-layouts: 7.16 us -> none
    another operation x2 -> x0, other arithmetic: 1.92 us -> none
    pallas_call x1, Pallas kernels: 8.95 us -> 10.6 us  [place(): pl.pallas_call(place_kernel, grid=(STEPS,), out_shape=(jax.ShapeDtypeStru...]
    broadcast_in_dim x1 -> x0, local copies, waits for them, and re-layouts: 1.34 us -> none  [on_device(): conv_bias[None]]
where the time goes in v4:
time: 124 us; the launch traced here: 123 us
  Pallas kernels  122 us (98%)
  between operations  1.29 us (1%)
    pallas_call x1, Pallas kernels, exchange(): pl.pallas_call(exchange_kernel, out_shape=out_shape, in_specs=[SM, SM, SM...  111 us
    pallas_call x1, Pallas kernels, place(): pl.pallas_call(place_kernel, grid=(STEPS,), out_shape=(jax.ShapeDtypeStru...  10.6 us

profile of v4, /device:TPU:1, one launch (start us, length us, event | category | flops | bytes accessed | tf_op | source)
XLA Modules:
  0.0 123.1 jit_solution(2908325612206961742)
XLA Ops:
  1.3 111.3 %exchange.1 = (bf16[13,1024,128]{2,1,0:T(8,128)(2,1)}, f32[15,32,128]{2,1,0:T(8,128)}, f32[1024,128]{1,0:T(8,128)}, bf16[512,4096]{1,0:T(8,128)(2,1)}, f32[512,128]{1,0:T(8,128)}) custom-call(s32[2,13]{1,0:T(2,128)} %bitcast.29, s32[13]{0:T(128)} %mask.1, s32[1]{0:T(128)S(6)} %copy.20.lens, f32[64]{0:T(128)} %skip.1, f32[13,1024,128]{2,1,0:T(8,128)} %bitcast.19, ...), custom_call_target="tpu_custom_call" | custom-call | tf_op jit(solution)/shard_map/exchange/pallas_call | solution.py:656
  112.6 10.6 %place.1 = (f32[13312,128]{1,0:T(8,128)}, bf16[512,4096]{1,0:T(8,128)(2,1)}, bf16[3,13,1024]{2,1,0:T(8,128)(2,1)}, bf16[3,13,64]{2,1,0:T(8,128)(2,1)}) custom-call(bf16[13312,128]{1,0:T(8,128)(2,1)} %bitcast.22, f32[1024,128]{1,0:T(8,128)} %get-tuple-element.14.fin, bf16[512,4096]{1,0:T(8,128)(2,1)} %get-tuple-element.15.gated, ...), custom_call_target="tpu_custom_call" | custom-call | tf_op jit(solution)/shard_map/place/pallas_call | solution.py:706

commit v5 on v4

--- a/solution.py
+++ b/solution.py
@@ -666,38 +666,42 @@
     )(*operands)
 
 
-STEPS = 8
+STEPS = 4
 PLACE_ROWS = SLOTS * 1024 // STEPS
 MIX_ROWS = SPAN // STEPS
 
 
 def place_kernel(moved, fin, gated, scale, norm_w, wout, states, mixed, win_in, win_st, acc_in, acc_st):
     my = lax.axis_index("seq")
+    step = pl.program_id(0)
     states[...] = moved[...].astype(F32)
 
-    @pl.when(pl.program_id(0) == 0)
+    @pl.when(step == 0)
     def _():
         states[pl.ds(0, 1024), :] = fin[...]
+
+    @pl.when(step < 3)
+    def _():
         for j in range(SLOTS):
             src = 0 if j == 0 else 2 + j
-            for i in range(3):
-                for q in range(8):
-                    acc_in[i, pl.ds(j, 1), pl.ds(q * 128, 128)] = wout[src, pl.ds(i * 8 + q, 1), :]
-                if j == 0:
-                    acc_st[i, pl.ds(0, 1), :] = jnp.where(my >= 2, wout[2, pl.ds(3 + i, 1), :], wout[1, pl.ds(3 + i, 1), :])
-                else:
-                    acc_st[i, pl.ds(j, 1), :] = wout[src, pl.ds(29 + i, 1), :]
-        for i in range(3):
-            win_in[i] = acc_in[i].astype(BF16)
-            rows = acc_st[i]
-            win_st[i] = jnp.where(my % 2 == 1, rows[:, 64:128], rows[:, 0:64]).astype(BF16)
+            for q in range(8):
+                acc_in[pl.ds(j, 1), pl.ds(q * 128, 128)] = wout[src, pl.ds(step * 8 + q, 1), :]
+            if j == 0:
+                row = pl.ds(3 + step, 1)
+                acc_st[pl.ds(0, 1), :] = jnp.where(my >= 2, wout[2, row, :], wout[1, row, :])
+            else:
+                acc_st[pl.ds(j, 1), :] = wout[src, pl.ds(29 + step, 1), :]
+        win_in[step] = acc_in[...].astype(BF16)
+        rows = acc_st[...]
+        win_st[step] = jnp.where(my % 2 == 1, rows[:, 64:128], rows[:, 0:64]).astype(BF16)
 
     def norm_body(i, carry):
-        lanes = pl.ds(pl.multiple_of(i * 128, 128), 128)
-        mixed[:, lanes] = (gated[:, lanes].astype(F32) * scale[...] * norm_w[pl.ds(i, 1), :]).astype(BF16)
+        span = pl.ds(pl.multiple_of(i * 16, 16), 16)
+        wide = jnp.concatenate([scale[span, :]] * PAIRS, axis=1)
+        mixed[span, :] = (gated[span, :].astype(F32) * wide * norm_w[0:1, :]).astype(BF16)
         return carry
 
-    lax.fori_loop(0, PAIRS, norm_body, 0, unroll=4)
+    lax.fori_loop(0, MIX_ROWS // 16, norm_body, 0)
 
 
 def place(moved, fin, gated, scale, norm_w, wout):
@@ -714,7 +718,7 @@
         ),
         in_specs=[rows(PLACE_ROWS, 128), VM, rows(MIX_ROWS, INNER), rows(MIX_ROWS, 128), VM, VM],
         out_specs=[rows(PLACE_ROWS, 128), rows(MIX_ROWS, INNER), whole(1024), whole(64)],
-        scratch_shapes=[pltpu.VMEM((3, SLOTS, 1024), F32), pltpu.VMEM((3, SLOTS, 128), F32)],
+        scratch_shapes=[pltpu.VMEM((SLOTS, 1024), F32), pltpu.VMEM((SLOTS, 128), F32)],
         name="place",
     )(moved, fin, gated, scale, norm_w, wout)
 
@@ -730,7 +734,7 @@
         conv_weight, conv_bias.reshape(34, 128), step_bias[None], decay_log[None],
     )
     new_states, mix, new_in, new_st = place(
-        moved.reshape(SLOTS * 1024, 128), fin, gated, scale, norm_weight.reshape(32, 128), wout)
+        moved.reshape(SLOTS * 1024, 128), fin, gated, scale, norm_weight[None], wout)
     return (
         new_states.reshape(SLOTS, 16, 64, 128), jnp.transpose(new_in, (1, 0, 2)), jnp.transpose(new_st, (1, 0, 2)),
         mix[None],

time: 124 us -> 121 us (0.976)
  Pallas kernels: 122 us -> 120 us
    pallas_call x1, Pallas kernels: 10.6 us -> 8.69 us  [place(): pl.pallas_call(place_kernel, grid=(STEPS,), out_shape=(jax.ShapeDtypeStru...]
where the time goes in v5:
time: 121 us
  Pallas kernels  120 us (99%)
  between operations  1.29 us (1%)
    pallas_call x1, Pallas kernels, exchange(): pl.pallas_call(exchange_kernel, out_shape=out_shape, in_specs=[SM, SM, SM...  111 us
    pallas_call x1, Pallas kernels, place(): pl.pallas_call(place_kernel, grid=(STEPS,), out_shape=(jax.ShapeDtypeStru...  8.69 us

profile of v5, /device:TPU:1, one launch (start us, length us, event | category | flops | bytes accessed | tf_op | source)
XLA Modules:
  0.0 121.2 jit_solution(16867554896251049837)
XLA Ops:
  1.3 111.3 %exchange.1 = (bf16[13,1024,128]{2,1,0:T(8,128)(2,1)}, f32[15,32,128]{2,1,0:T(8,128)}, f32[1024,128]{1,0:T(8,128)}, bf16[512,4096]{1,0:T(8,128)(2,1)}, f32[512,128]{1,0:T(8,128)}) custom-call(s32[2,13]{1,0:T(2,128)} %bitcast.29, s32[13]{0:T(128)} %mask.1, s32[1]{0:T(128)S(6)} %copy.20.lens, f32[64]{0:T(128)} %skip.1, f32[13,1024,128]{2,1,0:T(8,128)} %bitcast.19, ...), custom_call_target="tpu_custom_call" | custom-call | tf_op jit(solution)/shard_map/exchange/pallas_call | solution.py:656
  112.6 8.7 %place.1 = (f32[13312,128]{1,0:T(8,128)}, bf16[512,4096]{1,0:T(8,128)(2,1)}, bf16[3,13,1024]{2,1,0:T(8,128)(2,1)}, bf16[3,13,64]{2,1,0:T(8,128)(2,1)}) custom-call(bf16[13312,128]{1,0:T(8,128)(2,1)} %bitcast.22, f32[1024,128]{1,0:T(8,128)} %get-tuple-element.14.fin, bf16[512,4096]{1,0:T(8,128)(2,1)} %get-tuple-element.15.gated, ...), custom_call_target="tpu_custom_call" | custom-call | tf_op jit(solution)/shard_map/place/pallas_call | solution.py:710
